TPU v7x, 256 devices: a 4x2x16 block of a 4x16x16 slice. The times are simulated.
256 devices in a mesh: band: 2 (over y), coarse: 8 (over x, core), fine: 16 (over z).
Axes of the slice: x: 4, y: 2, z: 16, core: 2. Of those that a mesh axis runs over, the one named last changes fastest.
The devices are a block of a 4x16x16 slice.
Arguments:
- spectra: float32 [32, 16, 32768], P(None, ('band', 'coarse'), 'fine'), parts along dimension 1, may hold values from 0.2 to 5
Outputs:
- drift_power: float32 [8, 32, 16, 32768], P(None, None, ('band', 'coarse'), 'fine'), parts along dimension 2
There are 2 independent parts, one for each index of `band`. A program takes and returns all parts, laid end to end along the dimension named above; each array names one. Nothing has to cross between parts.
All inputs are finite; a program needn't handle non-finite values.
Results may differ from a plain program's by a relative error of at most 0.00002.
Values sent between devices are 32-bit elements; how exact they have to be, the bound alone decides.
No kernel may reach another device: no remote copies, remote signals or barrier semaphores. Data moves between devices by JAX's collectives and lax.ppermute only.
A program may use at most 64 MiB of HBM per device.

v0:
```python
import functools

import jax
import jax.numpy as jnp
from jax import lax
from jax.experimental import pallas as pl
from jax.experimental.pallas import tpu as pltpu
from jax.sharding import PartitionSpec as P


RATES = 8
LANES = 128
SUB = 8
VMEM_LIMIT = 36 * 1024 * 1024
APART = (1, 2, 3)
INSIDE_FLOPS = 40_000_000


def reverse(i, bits):
    return int(format(i, f"0{bits}b")[::-1], 2)


def plan(rows):
    half, levels, m = RATES // 2, [], 1
    while m < rows:
        size = 2 * m
        level = []
        for key in range(-half * (size - 1), half * (size - 1) + 1):
            q = min(key // (size - 1), half - 1)
            d = key - q * (size - 1)
            level.append((key, q * (m - 1) + d // 2, q * m + d - d // 2))
        levels.append((m, level))
        m = size
    return levels


def inside(rows, chunks, channels):
    half = RATES // 2
    levels = plan(rows)
    bits = len(levels)
    wide = chunks + 2

    def up(n):
        return -(-n // SUB) * SUB

    heights = [up((rows >> lv) * wide) + SUB for lv in range(bits)]
    counts = [2 * half * ((1 << lv) - 1) + 1 for lv in range(bits)]

    def at(start):
        return pl.ds(start, SUB)

    def kernel(x_ref, low_ref, high_ref, end_ref, stage, fixed, *bufs):
        trees, turns = bufs[:bits], bufs[bits:]
        lane = lax.broadcasted_iota(jnp.int32, (SUB, LANES), 1)
        line = lane + LANES * lax.broadcasted_iota(jnp.int32, (SUB, LANES), 0)

        none = jnp.zeros((1, LANES), jnp.float32)
        base = trees[0]
        for t in range(rows):
            r = reverse(t, bits) * wide
            base[0, pl.ds(r, 1), :] = none
            for k in range(0, chunks, SUB):
                sums = low_ref if k < chunks // 2 else high_ref
                inverse = 1.0 / (sums[t, at(k % (chunks // 2)), :] / channels)
                base[0, at(r + 1 + k), :] = x_ref[t, at(k), :] * inverse - 1.0
            base[0, pl.ds(r + 1 + chunks, 1), :] = none

        def grow(lv, m, level):
            src, dst, turn = trees[lv], trees[lv + 1], turns[lv]
            n = (rows >> (lv + 1)) * wide
            for w, (key, child, s) in enumerate(level):
                a, o = child + half * (m - 1), key + half * (2 * m - 1)
                if s:
                    for r in range(0, n, SUB):
                        turn[w, at(SUB + r), :] = pltpu.roll(src[a, at(n + r), :], -s % LANES, 1)
                for r in range(0, n, SUB):
                    if s == 0:
                        v = src[a, at(n + r), :]
                    elif s > 0:
                        v = lax.select(lane < LANES - s, turn[w, at(SUB + r), :], turn[w, at(SUB + r + 1), :])
                    else:
                        v = lax.select(lane >= -s, turn[w, at(SUB + r), :], turn[w, at(SUB + r - 1), :])
                    dst[o, at(r), :] = src[a, at(r), :] + v

        def apart(run):
            pl.when(end_ref[0] >= 0)(run)

        for lv, (m, level) in enumerate(levels[:-1]):
            step = functools.partial(grow, lv, m, level)
            if lv in APART:
                apart(step)
            else:
                step()

        m = levels[-1][0]
        src, turn = trees[-1], turns[-1]

        def finish(q):
            for d in range(rows):
                w = (q + half) * rows + d
                s = q * m + d - d // 2
                a = q * (m - 1) + d // 2 + half * (m - 1)
                vs = [src[a, at(wide + 1 + k), :] for k in range(0, chunks, SUB)]
                if s > 0:
                    vs[0] = lax.select(line < s, src[a, at(wide + 1 + chunks), :], vs[0])
                if s < 0:
                    vs[-1] = lax.select(line >= SUB * LANES + s, src[a, at(wide + 1 - SUB), :], vs[-1])
                if s:
                    vs = [pltpu.roll(v, -s % LANES, 1) for v in vs]
                    for i, v in enumerate(vs):
                        turn[w, at(SUB + SUB * i), :] = v
                    if s > 0:
                        turn[w, at(SUB + chunks), :] = vs[0]
                        vs = [lax.select(lane < LANES - s, v, turn[w, at(SUB + SUB * i + 1), :]) for i, v in enumerate(vs)]
                    else:
                        turn[w, at(0), :] = vs[-1]
                        vs = [lax.select(lane >= -s, v, turn[w, at(SUB + SUB * i - 1), :]) for i, v in enumerate(vs)]
                for i, v in enumerate(vs):
                    stage[w, at(SUB * i), :] = src[a, at(1 + SUB * i), :] + v

        @apart
        def _():
            for q in range(-half, 0):
                finish(q)

        @pl.when(end_ref[0] > 0)
        def _():
            rate = lax.broadcasted_iota(jnp.int32, (RATES, LANES), 0)
            slope = half - 1 - rate
            blocks = []
            for t in range(rows):
                r = reverse(t, bits) * wide + 1 + chunks
                parts = []
                for k in (2, 1):
                    v = base[0, pl.ds(r - k, 1), :]
                    if t:
                        v = pltpu.roll(v, LANES - (half - 1) * t, 1)
                    v = jnp.broadcast_to(v, (RATES, LANES))
                    step = t
                    if (RATES - 1) * t >= LANES:
                        v = pltpu.roll(v, 0, 1, stride=SUB * 2, stride_axis=0)
                        step = t - SUB * 2
                    if step:
                        v = pltpu.roll(v, 0, 1, stride=step, stride_axis=0)
                    parts.append(v)
                where = lane + slope * t
                v = jnp.where(where < 0, parts[0], jnp.where(where < LANES, parts[1], 0.0))
                blocks.append([v])
            while len(blocks) > 1:
                joined = []
                for first, second in zip(blocks[0::2], blocks[1::2]):
                    block = []
                    for d in range(2 * len(first)):
                        s, v = d - d // 2, second[d // 2]
                        if s:
                            v = jnp.where(lane < LANES - s, pltpu.roll(v, LANES - s, 1), 0.0)
                        block.append(first[d // 2] + v)
                    joined.append(block)
                blocks = joined
            for d in range(rows):
                fixed[...] = blocks[0][d]
                for q in range(-half, 0):
                    stage[(q + half) * rows + d, pl.ds(chunks - 1, 1), :] = fixed[pl.ds(half - 1 - q, 1), :]

        for q in range(half):
            finish(q)

    def call(x, low, high, end):
        f32 = jnp.float32
        paths = RATES * rows
        return pl.pallas_call(
            kernel,
            out_shape=jax.ShapeDtypeStruct((paths, chunks, LANES), f32),
            in_specs=[pl.BlockSpec(memory_space=pltpu.VMEM)] * 3 + [pl.BlockSpec(memory_space=pltpu.SMEM)],
            out_specs=pl.BlockSpec(memory_space=pltpu.VMEM),
            scratch_shapes=[pltpu.VMEM((RATES, LANES), f32)]
            + [pltpu.VMEM((counts[lv], heights[lv], LANES), f32) for lv in range(bits)]
            + [pltpu.VMEM((len(level), up((rows >> (lv + 1)) * wide) + 2 * SUB, LANES), f32) for lv, (_, level) in enumerate(levels[:-1])]
            + [pltpu.VMEM((paths, chunks + 2 * SUB, LANES), f32)],
            compiler_params=pltpu.CompilerParams(vmem_limit_bytes=VMEM_LIMIT),
            cost_estimate=pl.CostEstimate(flops=INSIDE_FLOPS, bytes_accessed=4 * paths * chunks * LANES, transcendentals=0),
            name="inside",
        )(x, low, high, end)

    return call


def edges(rows, chunks):
    half = RATES // 2
    levels = plan(rows)
    bits = len(levels)

    def up(n):
        return -(-n // SUB) * SUB

    def at(start):
        return pl.ds(start, SUB)

    heights = [up((rows >> lv) * 2) + SUB for lv in range(bits)]
    counts = [2 * half * ((1 << lv) - 1) + 2 for lv in range(bits)]

    def kernel(lo_ref, hi_ref, stage_ref, stage, out_ref, sems, *bufs):
        trees, turns = bufs[:bits], bufs[bits:]
        lane = lax.broadcasted_iota(jnp.int32, (SUB, LANES), 1)
        none = jnp.zeros((1, LANES), jnp.float32)
        for t in range(rows):
            r = 2 * reverse(t, bits)
            trees[0][0, pl.ds(r, 1), :] = lo_ref[pl.ds(t, 1), :]
            trees[0][0, pl.ds(r + 1, 1), :] = none
            trees[0][1, pl.ds(r, 1), :] = none
            trees[0][1, pl.ds(r + 1, 1), :] = hi_ref[pl.ds(t, 1), :]

        def place(key, m, above):
            return key + half * (m - 1) + above

        def shifted(turn, w, r, s):
            if s > 0:
                return lax.select(lane < LANES - s, turn[w, at(SUB + r), :], turn[w, at(SUB + r + 1), :])
            return lax.select(lane >= -s, turn[w, at(SUB + r), :], turn[w, at(SUB + r - 1), :])

        for lv, (m, level) in enumerate(levels[:-1]):
            src, dst, turn = trees[lv], trees[lv + 1], turns[lv]
            n = (rows >> (lv + 1)) * 2
            sides = [(key, child, s, 0) for key, child, s in level if key <= 0]
            sides += [(key, child, s, 1) for key, child, s in level if key >= 0]
            for key, child, s, above in sides:
                a, w = place(child, m, above), place(key, 2 * m, above)
                for r in range(0, n, SUB):
                    v = src[a, at(n + r), :]
                    if s:
                        turn[w, at(SUB + r), :] = pltpu.roll(v, -s % LANES, 1)
                for r in range(0, n, SUB):
                    v = shifted(turn, w, r, s) if s else src[a, at(n + r), :]
                    dst[w, at(r), :] = src[a, at(r), :] + v

        m = levels[-1][0]
        src, turn = trees[-1], turns[-1]
        copies = []
        for q in range(-half, half):
            above = int(q >= 0)
            for d in range(rows):
                w = (q + half) * rows + d
                s = q * m + d - d // 2
                a = place(q * (m - 1) + d // 2, m, above)
                v = src[a, at(2), :]
                if s:
                    turn[w, at(SUB), :] = pltpu.roll(v, -s % LANES, 1)
                    v = shifted(turn, w, 0, s)
                v = src[a, at(0), :] + v
                row, k = (0, chunks - 1) if above else (1, 0)
                stage[w, pl.ds(k, 1), :] = stage_ref[w, pl.ds(k, 1), :] + v[row : row + 1]
            part = pl.ds((q + half) * rows, rows)
            copy = pltpu.make_async_copy(stage.at[part], out_ref.at[part], sems.at[q + half])
            copy.start()
            copies.append(copy)
        for copy in copies:
            copy.wait()

    def call(lo, hi, stage):
        f32 = jnp.float32
        paths = RATES * rows
        shape = jax.ShapeDtypeStruct((paths, chunks, LANES), f32)
        return pl.pallas_call(
            kernel,
            out_shape=(shape, shape),
            in_specs=[pl.BlockSpec(memory_space=pltpu.VMEM)] * 3,
            out_specs=(pl.BlockSpec(memory_space=pltpu.VMEM), pl.BlockSpec(memory_space=pl.ANY)),
            scratch_shapes=[pltpu.SemaphoreType.DMA((RATES,))]
            + [pltpu.VMEM((counts[lv], heights[lv], LANES), f32) for lv in range(bits)]
            + [pltpu.VMEM((counts[lv + 1], up((rows >> (lv + 1)) * 2) + 2 * SUB, LANES), f32) for lv in range(bits - 1)]
            + [pltpu.VMEM((paths, 3 * SUB, LANES), f32)],
            input_output_aliases={2: 0},
            compiler_params=pltpu.CompilerParams(vmem_limit_bytes=VMEM_LIMIT),
            name="edges",
        )(lo, hi, stage)[1]

    return call


def exchange(value, axes, partner):
    pairs = [(i, partner(i)) for i in range(lax.axis_size(axes))]
    return lax.ppermute(value, axes, [(i, j) for i, j in pairs if j is not None])


def search(spectra):
    rows, _, columns = spectra.shape
    chunks = columns // LANES
    half = chunks // 2
    x = spectra.reshape(rows, chunks, LANES)
    channels = lax.axis_size("coarse") * spectra.shape[1]
    band, depth = ("coarse", "fine"), lax.axis_size("fine")
    place = lax.axis_index(band)
    side = lax.axis_index("coarse") % 2
    upper = side == 1

    own = jnp.where(upper, x[:, half:], x[:, :half])
    given = exchange(jnp.where(upper, x[:, :half], x[:, half:]), "coarse", lambda i: i ^ 1)
    total = own + given
    for near, far in ((2, 6), (6, 2)):
        total = total + exchange(total, "coarse", lambda i: i ^ (far if i % 2 else near))
    other = exchange(total, "coarse", lambda i: i ^ 1)

    def edge(v):
        return jnp.where(upper, v[:, -1], v[:, 0])

    inverse = 1.0 / (edge(total) / channels)
    mine, others = edge(own) * inverse - 1.0, edge(given) * inverse - 1.0
    at_turn = lax.axis_index("fine") == jnp.where(upper, depth - 1, 0)

    def along(i, cross):
        c, z = divmod(i, depth)
        step = 1 if c % 2 else -1
        if 0 <= z + step < depth:
            return (c ^ cross) * depth + z + step
        c += step * cross
        return c * depth + (z + step) % depth if 0 <= c < lax.axis_size("coarse") else None

    same = exchange(jnp.where(at_turn, others, mine), band, lambda i: along(i, 0))
    crossed = exchange(jnp.where(at_turn, mine, others), band, lambda i: along(i, 1))
    before, after = jnp.where(upper, same, crossed), jnp.where(upper, crossed, same)

    low, high = jnp.where(upper, other, total), jnp.where(upper, total, other)
    at_end = (place == lax.axis_size(band) - 1).astype(jnp.int32).reshape(1)
    stage = inside(rows, chunks, channels)(x, low, high, at_end)
    out = edges(rows, chunks)(before, after, stage)
    return out.reshape(RATES, rows, 1, columns)


def solution(mesh):
    in_specs = (P(None, ("band", "coarse"), "fine"),)
    out_specs = P(None, None, ("band", "coarse"), "fine")
    return jax.shard_map(search, mesh=mesh, in_specs=in_specs, out_specs=out_specs, check_vma=False)
```

profile of v0, /device:TPU:38, one launch (start us, length us, event | category | flops | bytes accessed | tf_op | source)
XLA Modules:
  0.0 50.0 jit_solution(1159648219855821853)
XLA Ops:
  0.0 0.0 copy-start
  0.0 1.0 %fusion.9 = (f32[32,8,128]{2,1,0:T(8,128)S(1)}, f32[32,8,128]{2,1,0:T(8,128)S(1)}) fusion(f32[32,16,128]{2,1,0:T(8,128)} %bitcast.7), kind=kLoop, calls=%fused_computation.18 | loop fusion | bytes 524288 | tf_op jit(solution)/shard_map/slice | solution.py:297
  1.1 0.1 collective-permute-start
  1.2 1.3 %collective-permute-done = f32[32,8,128]{2,0,1:T(8,128)S(1)} collective-permute-done((f32[32,8,128]{2,0,1:T(8,128)S(1)}, f32[32,8,128]{2,0,1:T(8,128)S(1)}, u32[]{:S(2)}, u32[]{:S(2)}) %collective-permute-start) | collective-permute-done | bytes 131104 | tf_op jit(solution)/shard_map/ppermute | solution.py:282
  2.6 0.1 fusion.8
  2.6 0.8 %collective-permute-start.1 = (f32[32,8,128]{2,0,1:T(8,128)S(1)}, f32[32,8,128]{2,0,1:T(8,128)S(1)}, u32[]{:S(2)}, u32[]{:S(2)}) collective-permute-start(f32[32,8,128]{2,0,1:T(8,128)S(1)} %get-tuple-element.10), channel_id=1, source_target_pairs={{0,32},{16,112},{32,0},{48,80},{64,96},{80,48},{96,64},{112,16},{1... | collective-permute-start | bytes 393224 | tf_op jit(solution)/shard_map/ppermute | solution.py:282
  3.4 4.3 %collective-permute-done.1 = f32[32,8,128]{2,0,1:T(8,128)S(1)} collective-permute-done((f32[32,8,128]{2,0,1:T(8,128)S(1)}, f32[32,8,128]{2,0,1:T(8,128)S(1)}, u32[]{:S(2)}, u32[]{:S(2)}) %collective-permute-start.1) | collective-permute-done | bytes 131104 | tf_op jit(solution)/shard_map/ppermute | solution.py:282
  7.7 19.2 %collective-permute-start.2 = (f32[32,8,128]{2,0,1:T(8,128)S(1)}, f32[32,8,128]{2,0,1:T(8,128)S(1)}, u32[]{:S(2)}, u32[]{:S(2)}) collective-permute-start(f32[32,8,128]{2,0,1:T(8,128)S(1)} %add.20), channel_id=1, source_target_pairs={{0,96},{16,48},{32,64},{48,16},{64,32},{80,112},{96,0},{112,80},{1... | collective-permute-start | bytes 393224 | tf_op jit(solution)/shard_map/ppermute | solution.py:282
  26.9 3.0 %collective-permute-done.2 = f32[32,8,128]{2,0,1:T(8,128)S(1)} collective-permute-done((f32[32,8,128]{2,0,1:T(8,128)S(1)}, f32[32,8,128]{2,0,1:T(8,128)S(1)}, u32[]{:S(2)}, u32[]{:S(2)}) %collective-permute-start.2) | collective-permute-done | bytes 131104 | tf_op jit(solution)/shard_map/ppermute | solution.py:282
  29.9 6.6 %collective-permute-start.3 = (f32[32,128]{1,0:T(8,128)S(1)}, f32[32,128]{1,0:T(8,128)S(1)}, u32[]{:S(2)}, u32[]{:S(2)}) collective-permute-start(f32[32,128]{1,0:T(8,128)S(1)} %select_bitcast_fusion.1), channel_id=1, source_target_pairs={{0,15},{1,0},{2,1},{3,2},{4,3},{5,4},{6,5},{7,6},{8,7},{9,8},{10,9... | collective-permute-start | bytes 49160 | tf_op jit(solution)/shard_map/ppermute | solution.py:282
  36.6 1.9 %collective-permute-start.4 = (f32[32,128]{1,0:T(8,128)S(1)}, f32[32,128]{1,0:T(8,128)S(1)}, u32[]{:S(2)}, u32[]{:S(2)}) collective-permute-start(f32[32,128]{1,0:T(8,128)S(1)} %get-tuple-element.7), channel_id=1, source_target_pairs={{1,16},{2,17},{3,18},{4,19},{5,20},{6,21},{7,22},{8,23},{9,24},{10... | collective-permute-start | bytes 49160 | tf_op jit(solution)/shard_map/ppermute | solution.py:282
  38.5 0.1 collective-permute-start.5
  38.7 0.0 collective-permute-done.3
  38.7 5.1 %collective-permute-done.4 = f32[32,128]{1,0:T(8,128)S(1)} collective-permute-done((f32[32,128]{1,0:T(8,128)S(1)}, f32[32,128]{1,0:T(8,128)S(1)}, u32[]{:S(2)}, u32[]{:S(2)}) %collective-permute-start.4) | collective-permute-done | bytes 16416 | tf_op jit(solution)/shard_map/ppermute | solution.py:282
  43.8 0.0 collective-permute-done.5
  43.8 0.1 copy.10.high_ref
  43.9 0.1 copy.9.low_ref
  44.0 0.0 copy-done
  44.0 3.9 %inside.1.stage_ref = f32[256,16,128]{2,1,0:T(8,128)S(1)} custom-call(f32[32,16,128]{2,1,0:T(8,128)S(1)} %bitcast.8, f32[32,8,128]{2,1,0:T(8,128)S(1)} %copy.9.low_ref, f32[32,8,128]{2,1,0:T(8,128)S(1)} %copy.10.high_ref, s32[1]{0:T(128)} %bitcast.3.end_ref), custom_call_target="tpu_custom_call" | custom-call | flops 40000000 | bytes 2097152 | tf_op jit(solution)/shard_map/inside/pallas_call | solution.py:171
  47.9 2.1 %edges.1 = (f32[256,16,128]{2,1,0:T(8,128)S(1)}, f32[256,16,128]{2,1,0:T(8,128)}) custom-call(f32[32,128]{1,0:T(8,128)S(1)} %get-tuple-element.17.lo_ref, f32[32,128]{1,0:T(8,128)S(1)} %get-tuple-element.16.hi_ref, f32[256,16,128]{2,1,0:T(8,128)S(1)} %inside.1.stage_ref), custom_call_target="tpu_custom_call", output_to_operand_aliasing={{0}: (2, {})} | custom-call | tf_op jit(solution)/shard_map/edges/pallas_call | solution.py:263
  (7 shorter events, 0.1 us)
Async XLA Ops:
  0.0 44.0 %copy-start = (f32[32,1,2048]{2,1,0:T(1,128)S(1)}, f32[32,1,2048]{2,1,0:T(1,128)}, u32[]{:S(2)}) copy-start(f32[32,1,2048]{2,1,0:T(1,128)} %param.1) | copy-start | bytes 786436
  1.1 1.5 %collective-permute-start = (f32[32,8,128]{2,0,1:T(8,128)S(1)}, f32[32,8,128]{2,0,1:T(8,128)S(1)}, u32[]{:S(2)}, u32[]{:S(2)}) collective-permute-start(f32[32,8,128]{2,0,1:T(8,128)S(1)} %copy_select_fusion.1), channel_id=1, source_target_pairs={{0,16},{16,0},{32,48},{48,32},{64,80},{80,64},{96,112},{112,96},{1... | collective-permute-start | bytes 393224 | tf_op jit(solution)/shard_map/ppermute | solution.py:282
  2.6 5.1 %collective-permute-start.1 = (f32[32,8,128]{2,0,1:T(8,128)S(1)}, f32[32,8,128]{2,0,1:T(8,128)S(1)}, u32[]{:S(2)}, u32[]{:S(2)}) collective-permute-start(f32[32,8,128]{2,0,1:T(8,128)S(1)} %get-tuple-element.10), channel_id=1, source_target_pairs={{0,32},{16,112},{32,0},{48,80},{64,96},{80,48},{96,64},{112,16},{1... | collective-permute-start | bytes 393224 | tf_op jit(solution)/shard_map/ppermute | solution.py:282
  7.7 22.1 %collective-permute-start.2 = (f32[32,8,128]{2,0,1:T(8,128)S(1)}, f32[32,8,128]{2,0,1:T(8,128)S(1)}, u32[]{:S(2)}, u32[]{:S(2)}) collective-permute-start(f32[32,8,128]{2,0,1:T(8,128)S(1)} %add.20), channel_id=1, source_target_pairs={{0,96},{16,48},{32,64},{48,16},{64,32},{80,112},{96,0},{112,80},{1... | collective-permute-start | bytes 393224 | tf_op jit(solution)/shard_map/ppermute | solution.py:282
  29.9 8.8 %collective-permute-start.3 = (f32[32,128]{1,0:T(8,128)S(1)}, f32[32,128]{1,0:T(8,128)S(1)}, u32[]{:S(2)}, u32[]{:S(2)}) collective-permute-start(f32[32,128]{1,0:T(8,128)S(1)} %select_bitcast_fusion.1), channel_id=1, source_target_pairs={{0,15},{1,0},{2,1},{3,2},{4,3},{5,4},{6,5},{7,6},{8,7},{9,8},{10,9... | collective-permute-start | bytes 49160 | tf_op jit(solution)/shard_map/ppermute | solution.py:282
  36.6 7.2 %collective-permute-start.4 = (f32[32,128]{1,0:T(8,128)S(1)}, f32[32,128]{1,0:T(8,128)S(1)}, u32[]{:S(2)}, u32[]{:S(2)}) collective-permute-start(f32[32,128]{1,0:T(8,128)S(1)} %get-tuple-element.7), channel_id=1, source_target_pairs={{1,16},{2,17},{3,18},{4,19},{5,20},{6,21},{7,22},{8,23},{9,24},{10... | collective-permute-start | bytes 49160 | tf_op jit(solution)/shard_map/ppermute | solution.py:282
  38.5 5.2 %collective-permute-start.5 = (f32[32,8,128]{2,0,1:T(8,128)S(1)}, f32[32,8,128]{2,0,1:T(8,128)S(1)}, u32[]{:S(2)}, u32[]{:S(2)}) collective-permute-start(f32[32,8,128]{2,0,1:T(8,128)S(1)} %add.21), channel_id=1, source_target_pairs={{0,16},{16,0},{32,48},{48,32},{64,80},{80,64},{96,112},{112,96},{1... | collective-permute-start | bytes 393224 | tf_op jit(solution)/shard_map/ppermute | solution.py:282
where the time goes:
time: 50.1 us; the launch traced here: 50 us
  starting transfers between devices  28.9 us (58%)
  waiting for transfers between devices  13.6 us (27%)
  Pallas kernels  5.96 us (12%)
  local copies, waits for them, and re-layouts  1.2 us (2%)
    ppermute x6, starting transfers between devices, exchange(): lax.ppermute(value, axes, [(i, j) for i, j in pairs if j is not None])  28.9 us
    ppermute x6, waiting for transfers between devices, exchange(): lax.ppermute(value, axes, [(i, j) for i, j in pairs if j is not None])  13.6 us
    pallas_call x1, Pallas kernels, call(): pl.pallas_call(kernel, out_shape=jax.ShapeDtypeStruct((paths, chunks, LAN...  3.91 us
    pallas_call x1, Pallas kernels, call(): pl.pallas_call(kernel, out_shape=(shape, shape), in_specs=[pl.BlockSpec(m...  2.05 us
    slice x1, local copies, waits for them, and re-layouts, search(): x[:, :half]  1.03 us
  transfers between devices with their start and end apart: 6, of which 4 were waited for; matrix products, arithmetic and copies ran while one was open for 0% of the time, Pallas kernels for 0%

commit v1 on v0

--- a/solution.py
+++ b/solution.py
@@ -1,5 +1,3 @@
-import functools
-
 import jax
 import jax.numpy as jnp
 from jax import lax
@@ -12,7 +10,6 @@
 LANES = 128
 SUB = 8
 VMEM_LIMIT = 36 * 1024 * 1024
-APART = (1, 2, 3)
 INSIDE_FLOPS = 40_000_000
 
 
@@ -82,15 +79,8 @@
                         v = lax.select(lane >= -s, turn[w, at(SUB + r), :], turn[w, at(SUB + r - 1), :])
                     dst[o, at(r), :] = src[a, at(r), :] + v
 
-        def apart(run):
-            pl.when(end_ref[0] >= 0)(run)
-
         for lv, (m, level) in enumerate(levels[:-1]):
-            step = functools.partial(grow, lv, m, level)
-            if lv in APART:
-                apart(step)
-            else:
-                step()
+            grow(lv, m, level)
 
         m = levels[-1][0]
         src, turn = trees[-1], turns[-1]
@@ -118,10 +108,8 @@
                 for i, v in enumerate(vs):
                     stage[w, at(SUB * i), :] = src[a, at(1 + SUB * i), :] + v
 
-        @apart
-        def _():
-            for q in range(-half, 0):
-                finish(q)
+        for q in range(-half, 0):
+            finish(q)
 
         @pl.when(end_ref[0] > 0)
         def _():
@@ -288,41 +276,33 @@
     half = chunks // 2
     x = spectra.reshape(rows, chunks, LANES)
     channels = lax.axis_size("coarse") * spectra.shape[1]
-    band, depth = ("coarse", "fine"), lax.axis_size("fine")
+    band = ("coarse", "fine")
     place = lax.axis_index(band)
     side = lax.axis_index("coarse") % 2
     upper = side == 1
 
     own = jnp.where(upper, x[:, half:], x[:, :half])
-    given = exchange(jnp.where(upper, x[:, :half], x[:, half:]), "coarse", lambda i: i ^ 1)
-    total = own + given
+    total = own + exchange(jnp.where(upper, x[:, :half], x[:, half:]), "coarse", lambda i: i ^ 1)
+
+    count = lax.axis_size(band)
+    odd = place % 2 == 1
+    first, last, total = lax.optimization_barrier((x[:, 0], x[:, -1], total))
+    even_rim = exchange(jnp.where(odd, first, last), band, lambda i: i ^ 1)
+    odd_rim = exchange(jnp.where(odd, last, first), band, lambda i: (i + (1 if i % 2 else -1)) % count)
+    rim = jnp.stack([jnp.where(odd, even_rim, odd_rim), jnp.where(odd, odd_rim, even_rim)])
+    rim_sum = rim
+    for cross in (1, 2, 6):
+        rim_sum = rim_sum + exchange(rim_sum, "coarse", lambda i: i ^ cross)
+    inside_band = jnp.stack([place > 0, place < count - 1])[:, None, None]
+    rim = jnp.where(inside_band, rim * (1.0 / (rim_sum / channels)) - 1.0, 0.0)
+
     for near, far in ((2, 6), (6, 2)):
         total = total + exchange(total, "coarse", lambda i: i ^ (far if i % 2 else near))
     other = exchange(total, "coarse", lambda i: i ^ 1)
-
-    def edge(v):
-        return jnp.where(upper, v[:, -1], v[:, 0])
-
-    inverse = 1.0 / (edge(total) / channels)
-    mine, others = edge(own) * inverse - 1.0, edge(given) * inverse - 1.0
-    at_turn = lax.axis_index("fine") == jnp.where(upper, depth - 1, 0)
-
-    def along(i, cross):
-        c, z = divmod(i, depth)
-        step = 1 if c % 2 else -1
-        if 0 <= z + step < depth:
-            return (c ^ cross) * depth + z + step
-        c += step * cross
-        return c * depth + (z + step) % depth if 0 <= c < lax.axis_size("coarse") else None
-
-    same = exchange(jnp.where(at_turn, others, mine), band, lambda i: along(i, 0))
-    crossed = exchange(jnp.where(at_turn, mine, others), band, lambda i: along(i, 1))
-    before, after = jnp.where(upper, same, crossed), jnp.where(upper, crossed, same)
-
     low, high = jnp.where(upper, other, total), jnp.where(upper, total, other)
-    at_end = (place == lax.axis_size(band) - 1).astype(jnp.int32).reshape(1)
+    at_end = (place == count - 1).astype(jnp.int32).reshape(1)
     stage = inside(rows, chunks, channels)(x, low, high, at_end)
-    out = edges(rows, chunks)(before, after, stage)
+    out = edges(rows, chunks)(rim[0], rim[1], stage)
     return out.reshape(RATES, rows, 1, columns)
 
 

time: 50.1 us -> 51.1 us (1.020)
  the two profiles are of different devices: /device:TPU:38 before, /device:TPU:33 now
where the time goes in v1:
time: 51.1 us; the launch traced here: 50.9 us
  starting transfers between devices  32 us (63%)
  waiting for transfers between devices  10.3 us (20%)
  Pallas kernels  5.38 us (11%)
  other arithmetic  2.25 us (4%)
  local copies, waits for them, and re-layouts  1 us (2%)
    ppermute x9, starting transfers between devices, exchange(): lax.ppermute(value, axes, [(i, j) for i, j in pairs if j is not None])  32 us
    ppermute x9, waiting for transfers between devices, exchange(): lax.ppermute(value, axes, [(i, j) for i, j in pairs if j is not None])  10.3 us
    pallas_call x1, Pallas kernels, call(): pl.pallas_call(kernel, out_shape=jax.ShapeDtypeStruct((paths, chunks, LAN...  3.33 us
    pallas_call x1, Pallas kernels, call(): pl.pallas_call(kernel, out_shape=(shape, shape), in_specs=[pl.BlockSpec(m...  2.05 us
    select_n x1, other arithmetic, search(): jnp.where(upper, x[:, :half], x[:, half:])  1.03 us
  transfers between devices with their start and end apart: 9, of which 7 were waited for; matrix products, arithmetic and copies ran while one was open for 2% of the time, Pallas kernels for 0%

profile of v1, /device:TPU:33, one launch (start us, length us, event | category | flops | bytes accessed | tf_op | source)
XLA Modules:
  0.0 50.9 jit_solution(2396384971182006739)
XLA Ops:
  0.0 0.0 copy-start
  0.0 1.0 %slice_select_fusion = f32[32,8,128]{2,1,0:T(8,128)S(1)} fusion(f32[32,16,128]{2,1,0:T(8,128)} %bitcast.19, pred[]{:T(512)S(6)} %eq.13), kind=kLoop, calls=%fused_computation.1 | loop fusion | flops 32768 | bytes 393217 | tf_op jit(solution)/shard_map/jit(_where)/select_n | solution.py:285
  1.0 20.5 %collective-permute-start = (f32[32,8,128]{2,1,0:T(8,128)S(1)}, f32[32,8,128]{2,1,0:T(8,128)S(1)}, u32[]{:S(2)}, u32[]{:S(2)}) collective-permute-start(f32[32,8,128]{2,1,0:T(8,128)S(1)} %slice_select_fusion), channel_id=1, source_target_pairs={{0,16},{16,0},{32,48},{48,32},{64,80},{80,64},{96,112},{112,96},{1... | collective-permute-start | bytes 393224 | tf_op jit(solution)/shard_map/ppermute | solution.py:270
  21.6 1.0 %fusion.1 = (f32[32,1,128]{2,1,0:T(1,128)S(1)}, f32[32,1,128]{2,1,0:T(1,128)S(1)}) fusion(f32[32,16,128]{2,1,0:T(8,128)} %bitcast.20), kind=kLoop, calls=%fused_computation.14 | loop fusion | bytes 65536 | tf_op jit(solution)/shard_map/slice | solution.py:289
  22.6 0.0 collective-permute-done
  22.6 1.0 %select_add_fusion = f32[32,8,128]{2,1,0:T(8,128)S(1)} fusion(f32[32,8,128]{2,1,0:T(8,128)S(1)} %collective-permute-done, f32[32,16,128]{2,1,0:T(8,128)} %bitcast.21, pred[]{:T(512)S(6)} %eq.13), kind=kLoop, calls=%fused_computation | loop fusion | flops 65536 | bytes 524289 | tf_op jit(solution)/shard_map/add | solution.py:285
  23.6 0.1 collective-permute-start.1
  23.7 3.5 %collective-permute-start.2 = (f32[32,128]{1,0:T(8,128)S(1)}, f32[32,128]{1,0:T(8,128)S(1)}, u32[]{:S(2)}, u32[]{:S(2)}) collective-permute-start(f32[32,128]{1,0:T(8,128)S(1)} %get-tuple-element.22), channel_id=1, source_target_pairs={{0,127},{1,2},{2,1},{3,4},{4,3},{5,6},{6,5},{7,8},{8,7},{9,10},{10... | collective-permute-start | bytes 49160 | tf_op jit(solution)/shard_map/ppermute | solution.py:270
  27.2 0.0 collective-permute-done.1
  27.2 1.4 %collective-permute-done.2 = f32[32,128]{1,0:T(8,128)S(1)} collective-permute-done((f32[32,128]{1,0:T(8,128)S(1)}, f32[32,128]{1,0:T(8,128)S(1)}, u32[]{:S(2)}, u32[]{:S(2)}) %collective-permute-start.2) | collective-permute-done | bytes 16416 | tf_op jit(solution)/shard_map/ppermute | solution.py:270
  28.6 2.9 %collective-permute-start.3 = (f32[2,32,128]{2,1,0:T(8,128)S(1)}, f32[2,32,128]{2,1,0:T(8,128)S(1)}, u32[]{:S(2)}, u32[]{:S(2)}) collective-permute-start(f32[2,32,128]{2,1,0:T(8,128)S(1)} %pad_maximum_fusion), channel_id=1, source_target_pairs={{0,16},{16,0},{32,48},{48,32},{64,80},{80,64},{96,112},{112,96},{1... | collective-permute-start | bytes 98312 | tf_op jit(solution)/shard_map/ppermute | solution.py:270
  31.5 0.9 %collective-permute-done.3 = f32[2,32,128]{2,1,0:T(8,128)S(1)} collective-permute-done((f32[2,32,128]{2,1,0:T(8,128)S(1)}, f32[2,32,128]{2,1,0:T(8,128)S(1)}, u32[]{:S(2)}, u32[]{:S(2)}) %collective-permute-start.3) | collective-permute-done | bytes 32800 | tf_op jit(solution)/shard_map/ppermute | solution.py:270
  32.4 0.0 collective-permute-start.4
  32.4 0.8 %collective-permute-start.6 = (f32[32,8,128]{2,1,0:T(8,128)S(1)}, f32[32,8,128]{2,1,0:T(8,128)S(1)}, u32[]{:S(2)}, u32[]{:S(2)}) collective-permute-start(f32[32,8,128]{2,1,0:T(8,128)S(1)} %select_add_fusion), channel_id=1, source_target_pairs={{0,32},{16,112},{32,0},{48,80},{64,96},{80,48},{96,64},{112,16},{1... | collective-permute-start | bytes 393224 | tf_op jit(solution)/shard_map/ppermute | solution.py:270
  33.3 1.9 %collective-permute-done.4 = f32[2,32,128]{2,1,0:T(8,128)S(1)} collective-permute-done((f32[2,32,128]{2,1,0:T(8,128)S(1)}, f32[2,32,128]{2,1,0:T(8,128)S(1)}, u32[]{:S(2)}, u32[]{:S(2)}) %collective-permute-start.4) | collective-permute-done | bytes 32800 | tf_op jit(solution)/shard_map/ppermute | solution.py:270
  35.2 0.6 %collective-permute-start.5 = (f32[2,32,128]{2,1,0:T(8,128)S(1)}, f32[2,32,128]{2,1,0:T(8,128)S(1)}, u32[]{:S(2)}, u32[]{:S(2)}) collective-permute-start(f32[2,32,128]{2,1,0:T(8,128)S(1)} %fusion.2), channel_id=1, source_target_pairs={{0,96},{16,112},{32,64},{48,80},{64,32},{80,48},{96,0},{112,16},{1... | collective-permute-start | bytes 98312 | tf_op jit(solution)/shard_map/ppermute | solution.py:270
  35.8 0.1 pad_add_fusion
  35.8 1.7 %collective-permute-done.6 = f32[32,8,128]{2,1,0:T(8,128)S(1)} collective-permute-done((f32[32,8,128]{2,1,0:T(8,128)S(1)}, f32[32,8,128]{2,1,0:T(8,128)S(1)}, u32[]{:S(2)}, u32[]{:S(2)}) %collective-permute-start.6) | collective-permute-done | bytes 131104 | tf_op jit(solution)/shard_map/ppermute | solution.py:270
  37.6 0.5 %collective-permute-start.7 = (f32[32,8,128]{2,1,0:T(8,128)S(1)}, f32[32,8,128]{2,1,0:T(8,128)S(1)}, u32[]{:S(2)}, u32[]{:S(2)}) collective-permute-start(f32[32,8,128]{2,1,0:T(8,128)S(1)} %add.36), channel_id=1, source_target_pairs={{0,96},{16,48},{32,64},{48,16},{64,32},{80,112},{96,0},{112,80},{1... | collective-permute-start | bytes 393224 | tf_op jit(solution)/shard_map/ppermute | solution.py:270
  38.1 1.2 %collective-permute-done.5 = f32[2,32,128]{2,1,0:T(8,128)S(1)} collective-permute-done((f32[2,32,128]{2,1,0:T(8,128)S(1)}, f32[2,32,128]{2,1,0:T(8,128)S(1)}, u32[]{:S(2)}, u32[]{:S(2)}) %collective-permute-start.5) | collective-permute-done | bytes 32800 | tf_op jit(solution)/shard_map/ppermute | solution.py:270
  39.3 0.1 add_select_fusion
  39.4 2.2 %collective-permute-done.7 = f32[32,8,128]{2,1,0:T(8,128)S(1)} collective-permute-done((f32[32,8,128]{2,1,0:T(8,128)S(1)}, f32[32,8,128]{2,1,0:T(8,128)S(1)}, u32[]{:S(2)}, u32[]{:S(2)}) %collective-permute-start.7) | collective-permute-done | bytes 131104 | tf_op jit(solution)/shard_map/ppermute | solution.py:270
  41.6 3.0 %collective-permute-start.8 = (f32[32,8,128]{2,1,0:T(8,128)S(1)}, f32[32,8,128]{2,1,0:T(8,128)S(1)}, u32[]{:S(2)}, u32[]{:S(2)}) collective-permute-start(f32[32,8,128]{2,1,0:T(8,128)S(1)} %add.37), channel_id=1, source_target_pairs={{0,16},{16,0},{32,48},{48,32},{64,80},{80,64},{96,112},{112,96},{1... | collective-permute-start | bytes 393224 | tf_op jit(solution)/shard_map/ppermute | solution.py:270
  44.5 1.0 %collective-permute-done.8 = f32[32,8,128]{2,1,0:T(8,128)S(1)} collective-permute-done((f32[32,8,128]{2,1,0:T(8,128)S(1)}, f32[32,8,128]{2,1,0:T(8,128)S(1)}, u32[]{:S(2)}, u32[]{:S(2)}) %collective-permute-start.8) | collective-permute-done | bytes 131104 | tf_op jit(solution)/shard_map/ppermute | solution.py:270
  45.5 0.0 copy-done
  45.6 3.3 %inside.1.stage_ref = f32[256,16,128]{2,1,0:T(8,128)S(1)} custom-call(f32[32,16,128]{2,1,0:T(8,128)S(1)} %bitcast.22, f32[32,8,128]{2,1,0:T(8,128)S(1)} %get-tuple-element.14.low_ref, f32[32,8,128]{2,1,0:T(8,128)S(1)} %get-tuple-element.13.high_ref, s32[1]{0:T(128)} %bitcast.9.end_ref), custom_call_target="tpu_custom_call" | custom-call | flops 40000000 | bytes 2097152 | tf_op jit(solution)/shard_map/inside/pallas_call | solution.py:159
  48.9 2.1 %edges.1 = (f32[256,16,128]{2,1,0:T(8,128)S(1)}, f32[256,16,128]{2,1,0:T(8,128)}) custom-call(f32[32,128]{1,0:T(8,128)S(1)} %get-tuple-element.18.lo_ref, f32[32,128]{1,0:T(8,128)S(1)} %get-tuple-element.17.hi_ref, f32[256,16,128]{2,1,0:T(8,128)S(1)} %inside.1.stage_ref), custom_call_target="tpu_custom_call", output_to_operand_aliasing={{0}: (2, {})} | custom-call | tf_op jit(solution)/shard_map/edges/pallas_call | solution.py:251
  (9 shorter events, 0.1 us)
Async XLA Ops:
  0.0 45.5 %copy-start = (f32[32,1,2048]{2,1,0:T(1,128)S(1)}, f32[32,1,2048]{2,1,0:T(1,128)}, u32[]{:S(2)}) copy-start(f32[32,1,2048]{2,1,0:T(1,128)} %param.1) | copy-start | bytes 786436
  1.0 21.5 %collective-permute-start = (f32[32,8,128]{2,1,0:T(8,128)S(1)}, f32[32,8,128]{2,1,0:T(8,128)S(1)}, u32[]{:S(2)}, u32[]{:S(2)}) collective-permute-start(f32[32,8,128]{2,1,0:T(8,128)S(1)} %slice_select_fusion), channel_id=1, source_target_pairs={{0,16},{16,0},{32,48},{48,32},{64,80},{80,64},{96,112},{112,96},{1... | collective-permute-start | bytes 393224 | tf_op jit(solution)/shard_map/ppermute | solution.py:270
  23.6 3.6 %collective-permute-start.1 = (f32[32,128]{1,0:T(8,128)S(1)}, f32[32,128]{1,0:T(8,128)S(1)}, u32[]{:S(2)}, u32[]{:S(2)}) collective-permute-start(f32[32,128]{1,0:T(8,128)S(1)} %get-tuple-element.21), channel_id=1, source_target_pairs={{0,1},{1,0},{2,3},{3,2},{4,5},{5,4},{6,7},{7,6},{8,9},{9,8},{10,11... | collective-permute-start | bytes 49160 | tf_op jit(solution)/shard_map/ppermute | solution.py:270
  23.7 4.9 %collective-permute-start.2 = (f32[32,128]{1,0:T(8,128)S(1)}, f32[32,128]{1,0:T(8,128)S(1)}, u32[]{:S(2)}, u32[]{:S(2)}) collective-permute-start(f32[32,128]{1,0:T(8,128)S(1)} %get-tuple-element.22), channel_id=1, source_target_pairs={{0,127},{1,2},{2,1},{3,4},{4,3},{5,6},{6,5},{7,8},{8,7},{9,10},{10... | collective-permute-start | bytes 49160 | tf_op jit(solution)/shard_map/ppermute | solution.py:270
  28.6 3.8 %collective-permute-start.3 = (f32[2,32,128]{2,1,0:T(8,128)S(1)}, f32[2,32,128]{2,1,0:T(8,128)S(1)}, u32[]{:S(2)}, u32[]{:S(2)}) collective-permute-start(f32[2,32,128]{2,1,0:T(8,128)S(1)} %pad_maximum_fusion), channel_id=1, source_target_pairs={{0,16},{16,0},{32,48},{48,32},{64,80},{80,64},{96,112},{112,96},{1... | collective-permute-start | bytes 98312 | tf_op jit(solution)/shard_map/ppermute | solution.py:270
  32.4 2.8 %collective-permute-start.4 = (f32[2,32,128]{2,1,0:T(8,128)S(1)}, f32[2,32,128]{2,1,0:T(8,128)S(1)}, u32[]{:S(2)}, u32[]{:S(2)}) collective-permute-start(f32[2,32,128]{2,1,0:T(8,128)S(1)} %fusion), channel_id=1, source_target_pairs={{0,32},{16,48},{32,0},{48,16},{64,96},{80,112},{96,64},{112,80},{1... | collective-permute-start | bytes 98312 | tf_op jit(solution)/shard_map/ppermute | solution.py:270
  32.4 5.2 %collective-permute-start.6 = (f32[32,8,128]{2,1,0:T(8,128)S(1)}, f32[32,8,128]{2,1,0:T(8,128)S(1)}, u32[]{:S(2)}, u32[]{:S(2)}) collective-permute-start(f32[32,8,128]{2,1,0:T(8,128)S(1)} %select_add_fusion), channel_id=1, source_target_pairs={{0,32},{16,112},{32,0},{48,80},{64,96},{80,48},{96,64},{112,16},{1... | collective-permute-start | bytes 393224 | tf_op jit(solution)/shard_map/ppermute | solution.py:270
  35.2 4.1 %collective-permute-start.5 = (f32[2,32,128]{2,1,0:T(8,128)S(1)}, f32[2,32,128]{2,1,0:T(8,128)S(1)}, u32[]{:S(2)}, u32[]{:S(2)}) collective-permute-start(f32[2,32,128]{2,1,0:T(8,128)S(1)} %fusion.2), channel_id=1, source_target_pairs={{0,96},{16,112},{32,64},{48,80},{64,32},{80,48},{96,0},{112,16},{1... | collective-permute-start | bytes 98312 | tf_op jit(solution)/shard_map/ppermute | solution.py:270
  37.6 3.9 %collective-permute-start.7 = (f32[32,8,128]{2,1,0:T(8,128)S(1)}, f32[32,8,128]{2,1,0:T(8,128)S(1)}, u32[]{:S(2)}, u32[]{:S(2)}) collective-permute-start(f32[32,8,128]{2,1,0:T(8,128)S(1)} %add.36), channel_id=1, source_target_pairs={{0,96},{16,48},{32,64},{48,16},{64,32},{80,112},{96,0},{112,80},{1... | collective-permute-start | bytes 393224 | tf_op jit(solution)/shard_map/ppermute | solution.py:270
  41.6 4.0 %collective-permute-start.8 = (f32[32,8,128]{2,1,0:T(8,128)S(1)}, f32[32,8,128]{2,1,0:T(8,128)S(1)}, u32[]{:S(2)}, u32[]{:S(2)}) collective-permute-start(f32[32,8,128]{2,1,0:T(8,128)S(1)} %add.37), channel_id=1, source_target_pairs={{0,16},{16,0},{32,48},{48,32},{64,80},{80,64},{96,112},{112,96},{1... | collective-permute-start | bytes 393224 | tf_op jit(solution)/shard_map/ppermute | solution.py:270

commit v2 on v1

--- a/solution.py
+++ b/solution.py
@@ -281,22 +281,25 @@
     side = lax.axis_index("coarse") % 2
     upper = side == 1
 
-    own = jnp.where(upper, x[:, half:], x[:, :half])
-    total = own + exchange(jnp.where(upper, x[:, :half], x[:, half:]), "coarse", lambda i: i ^ 1)
+    own, given = lax.optimization_barrier(
+        (jnp.where(upper, x[:, half:], x[:, :half]), jnp.where(upper, x[:, :half], x[:, half:]))
+    )
+    total = own + exchange(given, "coarse", lambda i: i ^ 1)
 
     count = lax.axis_size(band)
     odd = place % 2 == 1
-    first, last, total = lax.optimization_barrier((x[:, 0], x[:, -1], total))
+    first = jnp.where(upper, given[:, 0], own[:, 0])
+    last = jnp.where(upper, own[:, -1], given[:, -1])
     even_rim = exchange(jnp.where(odd, first, last), band, lambda i: i ^ 1)
     odd_rim = exchange(jnp.where(odd, last, first), band, lambda i: (i + (1 if i % 2 else -1)) % count)
     rim = jnp.stack([jnp.where(odd, even_rim, odd_rim), jnp.where(odd, odd_rim, even_rim)])
     rim_sum = rim
-    for cross in (1, 2, 6):
+    for cross in (1, 6, 2):
         rim_sum = rim_sum + exchange(rim_sum, "coarse", lambda i: i ^ cross)
     inside_band = jnp.stack([place > 0, place < count - 1])[:, None, None]
     rim = jnp.where(inside_band, rim * (1.0 / (rim_sum / channels)) - 1.0, 0.0)
 
-    for near, far in ((2, 6), (6, 2)):
+    for near, far in ((6, 2), (2, 6)):
         total = total + exchange(total, "coarse", lambda i: i ^ (far if i % 2 else near))
     other = exchange(total, "coarse", lambda i: i ^ 1)
     low, high = jnp.where(upper, other, total), jnp.where(upper, total, other)

time: 51.1 us -> 49.2 us (0.963)
  other arithmetic: 2.25 us -> 0.31 us
    select_n x1, other arithmetic: 1.03 us -> 0.05 us  [search(): jnp.where(upper, x[:, :half], x[:, half:])]
    add x1, other arithmetic: 0.99 us -> 0.02 us  [search(): total = own + exchange(given, 'coarse', lambda i: i ^ 1)]
  transfers between devices with their start and end apart: 9 -> 9, of which waited for: 7 -> 7; matrix products, arithmetic and copies ran while one was open for 2% -> 0% of each run, Pallas kernels for 0% -> 0%
where the time goes in v2:
time: 49.2 us; the launch traced here: 49.1 us
  starting transfers between devices  31.8 us (65%)
  waiting for transfers between devices  10.3 us (21%)
  Pallas kernels  5.38 us (11%)
  local copies, waits for them, and re-layouts  1.2 us (2%)
    ppermute x9, starting transfers between devices, exchange(): lax.ppermute(value, axes, [(i, j) for i, j in pairs if j is not None])  31.8 us
    ppermute x9, waiting for transfers between devices, exchange(): lax.ppermute(value, axes, [(i, j) for i, j in pairs if j is not None])  10.3 us
    pallas_call x1, Pallas kernels, call(): pl.pallas_call(kernel, out_shape=jax.ShapeDtypeStruct((paths, chunks, LAN...  3.33 us
    pallas_call x1, Pallas kernels, call(): pl.pallas_call(kernel, out_shape=(shape, shape), in_specs=[pl.BlockSpec(m...  2.05 us
    slice x1, local copies, waits for them, and re-layouts, search(): x[:, half:]  1.03 us
  transfers between devices with their start and end apart: 9, of which 7 were waited for; matrix products, arithmetic and copies ran while one was open for 0% of the time, Pallas kernels for 0%

profile of v2, /device:TPU:33, one launch (start us, length us, event | category | flops | bytes accessed | tf_op | source)
XLA Modules:
  0.0 49.1 jit_solution(10276319148557880678)
XLA Ops:
  0.0 0.0 copy-start
  0.0 1.0 %fusion.1 = (f32[32,8,128]{2,1,0:T(8,128)S(1)}, f32[32,8,128]{2,1,0:T(8,128)S(1)}) fusion(f32[32,16,128]{2,1,0:T(8,128)} %bitcast.17), kind=kLoop, calls=%fused_computation.16 | loop fusion | bytes 524288 | tf_op jit(solution)/shard_map/slice | solution.py:285
  1.1 3.4 %collective-permute-start = (f32[32,128]{1,0:T(8,128)S(1)}, f32[32,128]{1,0:T(8,128)S(1)}, u32[]{:S(2)}, u32[]{:S(2)}) collective-permute-start(f32[32,128]{1,0:T(8,128)S(1)} %get-tuple-element.13), channel_id=1, source_target_pairs={{0,1},{1,0},{2,3},{3,2},{4,5},{5,4},{6,7},{7,6},{8,9},{9,8},{10,11... | collective-permute-start | bytes 49160 | tf_op jit(solution)/shard_map/ppermute | solution.py:270
  4.5 20.2 %collective-permute-start.1 = (f32[32,128]{1,0:T(8,128)S(1)}, f32[32,128]{1,0:T(8,128)S(1)}, u32[]{:S(2)}, u32[]{:S(2)}) collective-permute-start(f32[32,128]{1,0:T(8,128)S(1)} %get-tuple-element.14), channel_id=1, source_target_pairs={{0,127},{1,2},{2,1},{3,4},{4,3},{5,6},{6,5},{7,8},{8,7},{9,10},{10... | collective-permute-start | bytes 49160 | tf_op jit(solution)/shard_map/ppermute | solution.py:270
  24.8 0.0 collective-permute-done
  24.8 1.4 %collective-permute-done.1 = f32[32,128]{1,0:T(8,128)S(1)} collective-permute-done((f32[32,128]{1,0:T(8,128)S(1)}, f32[32,128]{1,0:T(8,128)S(1)}, u32[]{:S(2)}, u32[]{:S(2)}) %collective-permute-start.1) | collective-permute-done | bytes 16416 | tf_op jit(solution)/shard_map/ppermute | solution.py:270
  26.2 2.6 %collective-permute-start.2 = (f32[2,32,128]{2,1,0:T(8,128)S(1)}, f32[2,32,128]{2,1,0:T(8,128)S(1)}, u32[]{:S(2)}, u32[]{:S(2)}) collective-permute-start(f32[2,32,128]{2,1,0:T(8,128)S(1)} %pad_maximum_fusion), channel_id=1, source_target_pairs={{0,16},{16,0},{32,48},{48,32},{64,80},{80,64},{96,112},{112,96},{1... | collective-permute-start | bytes 98312 | tf_op jit(solution)/shard_map/ppermute | solution.py:270
  28.9 0.1 collective-permute-start.5
  29.0 0.7 %collective-permute-done.2 = f32[2,32,128]{2,1,0:T(8,128)S(1)} collective-permute-done((f32[2,32,128]{2,1,0:T(8,128)S(1)}, f32[2,32,128]{2,1,0:T(8,128)S(1)}, u32[]{:S(2)}, u32[]{:S(2)}) %collective-permute-start.2) | collective-permute-done | bytes 32800 | tf_op jit(solution)/shard_map/ppermute | solution.py:270
  29.7 0.7 %collective-permute-start.3 = (f32[2,32,128]{2,1,0:T(8,128)S(1)}, f32[2,32,128]{2,1,0:T(8,128)S(1)}, u32[]{:S(2)}, u32[]{:S(2)}) collective-permute-start(f32[2,32,128]{2,1,0:T(8,128)S(1)} %fusion), channel_id=1, source_target_pairs={{0,96},{16,112},{32,64},{48,80},{64,32},{80,48},{96,0},{112,16},{1... | collective-permute-start | bytes 98312 | tf_op jit(solution)/shard_map/ppermute | solution.py:270
  30.5 0.0 collective-permute-done.5
  30.5 0.1 collective-permute-start.6
  30.6 3.1 %collective-permute-done.3 = f32[2,32,128]{2,1,0:T(8,128)S(1)} collective-permute-done((f32[2,32,128]{2,1,0:T(8,128)S(1)}, f32[2,32,128]{2,1,0:T(8,128)S(1)}, u32[]{:S(2)}, u32[]{:S(2)}) %collective-permute-start.3) | collective-permute-done | bytes 32800 | tf_op jit(solution)/shard_map/ppermute | solution.py:270
  33.7 0.1 collective-permute-start.4
  33.9 0.1 pad_add_fusion
  34.0 0.8 %collective-permute-done.6 = f32[32,8,128]{2,0,1:T(8,128)S(1)} collective-permute-done((f32[32,8,128]{2,0,1:T(8,128)S(1)}, f32[32,8,128]{2,0,1:T(8,128)S(1)}, u32[]{:S(2)}, u32[]{:S(2)}) %collective-permute-start.6) | collective-permute-done | bytes 131104 | tf_op jit(solution)/shard_map/ppermute | solution.py:270
  34.7 1.8 %collective-permute-start.7 = (f32[32,8,128]{2,0,1:T(8,128)S(1)}, f32[32,8,128]{2,0,1:T(8,128)S(1)}, u32[]{:S(2)}, u32[]{:S(2)}) collective-permute-start(f32[32,8,128]{2,0,1:T(8,128)S(1)} %add.36), channel_id=1, source_target_pairs={{0,32},{16,112},{32,0},{48,80},{64,96},{80,48},{96,64},{112,16},{1... | collective-permute-start | bytes 393224 | tf_op jit(solution)/shard_map/ppermute | solution.py:270
  36.5 0.3 collective-permute-done.4
  36.8 0.1 add_select_fusion
  36.9 3.0 %collective-permute-done.7 = f32[32,8,128]{2,0,1:T(8,128)S(1)} collective-permute-done((f32[32,8,128]{2,0,1:T(8,128)S(1)}, f32[32,8,128]{2,0,1:T(8,128)S(1)}, u32[]{:S(2)}, u32[]{:S(2)}) %collective-permute-start.7) | collective-permute-done | bytes 131104 | tf_op jit(solution)/shard_map/ppermute | solution.py:270
  39.9 2.6 %collective-permute-start.8 = (f32[32,8,128]{2,0,1:T(8,128)S(1)}, f32[32,8,128]{2,0,1:T(8,128)S(1)}, u32[]{:S(2)}, u32[]{:S(2)}) collective-permute-start(f32[32,8,128]{2,0,1:T(8,128)S(1)} %add.37), channel_id=1, source_target_pairs={{0,16},{16,0},{32,48},{48,32},{64,80},{80,64},{96,112},{112,96},{1... | collective-permute-start | bytes 393224 | tf_op jit(solution)/shard_map/ppermute | solution.py:270
  42.5 1.0 %collective-permute-done.8 = f32[32,8,128]{2,0,1:T(8,128)S(1)} collective-permute-done((f32[32,8,128]{2,0,1:T(8,128)S(1)}, f32[32,8,128]{2,0,1:T(8,128)S(1)}, u32[]{:S(2)}, u32[]{:S(2)}) %collective-permute-start.8) | collective-permute-done | bytes 131104 | tf_op jit(solution)/shard_map/ppermute | solution.py:270
  43.5 0.1 copy.10.high_ref
  43.6 0.1 copy.9.low_ref
  43.7 0.0 copy-done
  43.7 3.3 %inside.1.stage_ref = f32[256,16,128]{2,1,0:T(8,128)S(1)} custom-call(f32[32,16,128]{2,1,0:T(8,128)S(1)} %bitcast.18, f32[32,8,128]{2,1,0:T(8,128)S(1)} %copy.9.low_ref, f32[32,8,128]{2,1,0:T(8,128)S(1)} %copy.10.high_ref, s32[1]{0:T(128)} %bitcast.9.end_ref), custom_call_target="tpu_custom_call" | custom-call | flops 40000000 | bytes 2097152 | tf_op jit(solution)/shard_map/inside/pallas_call | solution.py:159
  47.0 2.1 %edges.1 = (f32[256,16,128]{2,1,0:T(8,128)S(1)}, f32[256,16,128]{2,1,0:T(8,128)}) custom-call(f32[32,128]{1,0:T(8,128)S(1)} %get-tuple-element.20.lo_ref, f32[32,128]{1,0:T(8,128)S(1)} %get-tuple-element.19.hi_ref, f32[256,16,128]{2,1,0:T(8,128)S(1)} %inside.1.stage_ref), custom_call_target="tpu_custom_call", output_to_operand_aliasing={{0}: (2, {})} | custom-call | tf_op jit(solution)/shard_map/edges/pallas_call | solution.py:251
  (11 shorter events, 0.2 us)
Async XLA Ops:
  0.0 43.7 %copy-start = (f32[32,1,2048]{2,1,0:T(1,128)S(1)}, f32[32,1,2048]{2,1,0:T(1,128)}, u32[]{:S(2)}) copy-start(f32[32,1,2048]{2,1,0:T(1,128)} %param.1) | copy-start | bytes 786436
  1.1 23.7 %collective-permute-start = (f32[32,128]{1,0:T(8,128)S(1)}, f32[32,128]{1,0:T(8,128)S(1)}, u32[]{:S(2)}, u32[]{:S(2)}) collective-permute-start(f32[32,128]{1,0:T(8,128)S(1)} %get-tuple-element.13), channel_id=1, source_target_pairs={{0,1},{1,0},{2,3},{3,2},{4,5},{5,4},{6,7},{7,6},{8,9},{9,8},{10,11... | collective-permute-start | bytes 49160 | tf_op jit(solution)/shard_map/ppermute | solution.py:270
  4.5 21.7 %collective-permute-start.1 = (f32[32,128]{1,0:T(8,128)S(1)}, f32[32,128]{1,0:T(8,128)S(1)}, u32[]{:S(2)}, u32[]{:S(2)}) collective-permute-start(f32[32,128]{1,0:T(8,128)S(1)} %get-tuple-element.14), channel_id=1, source_target_pairs={{0,127},{1,2},{2,1},{3,4},{4,3},{5,6},{6,5},{7,8},{8,7},{9,10},{10... | collective-permute-start | bytes 49160 | tf_op jit(solution)/shard_map/ppermute | solution.py:270
  26.2 3.5 %collective-permute-start.2 = (f32[2,32,128]{2,1,0:T(8,128)S(1)}, f32[2,32,128]{2,1,0:T(8,128)S(1)}, u32[]{:S(2)}, u32[]{:S(2)}) collective-permute-start(f32[2,32,128]{2,1,0:T(8,128)S(1)} %pad_maximum_fusion), channel_id=1, source_target_pairs={{0,16},{16,0},{32,48},{48,32},{64,80},{80,64},{96,112},{112,96},{1... | collective-permute-start | bytes 98312 | tf_op jit(solution)/shard_map/ppermute | solution.py:270
  28.9 1.6 %collective-permute-start.5 = (f32[32,8,128]{2,0,1:T(8,128)S(1)}, f32[32,8,128]{2,0,1:T(8,128)S(1)}, u32[]{:S(2)}, u32[]{:S(2)}) collective-permute-start(f32[32,8,128]{2,0,1:T(8,128)S(1)} %get-tuple-element.8), channel_id=1, source_target_pairs={{0,16},{16,0},{32,48},{48,32},{64,80},{80,64},{96,112},{112,96},{1... | collective-permute-start | bytes 393224 | tf_op jit(solution)/shard_map/ppermute | solution.py:270
  29.7 4.0 %collective-permute-start.3 = (f32[2,32,128]{2,1,0:T(8,128)S(1)}, f32[2,32,128]{2,1,0:T(8,128)S(1)}, u32[]{:S(2)}, u32[]{:S(2)}) collective-permute-start(f32[2,32,128]{2,1,0:T(8,128)S(1)} %fusion), channel_id=1, source_target_pairs={{0,96},{16,112},{32,64},{48,80},{64,32},{80,48},{96,0},{112,16},{1... | collective-permute-start | bytes 98312 | tf_op jit(solution)/shard_map/ppermute | solution.py:270
  30.5 4.2 %collective-permute-start.6 = (f32[32,8,128]{2,0,1:T(8,128)S(1)}, f32[32,8,128]{2,0,1:T(8,128)S(1)}, u32[]{:S(2)}, u32[]{:S(2)}) collective-permute-start(f32[32,8,128]{2,0,1:T(8,128)S(1)} %add.35), channel_id=1, source_target_pairs={{0,96},{16,48},{32,64},{48,16},{64,32},{80,112},{96,0},{112,80},{1... | collective-permute-start | bytes 393224 | tf_op jit(solution)/shard_map/ppermute | solution.py:270
  33.7 3.1 %collective-permute-start.4 = (f32[2,32,128]{2,1,0:T(8,128)S(1)}, f32[2,32,128]{2,1,0:T(8,128)S(1)}, u32[]{:S(2)}, u32[]{:S(2)}) collective-permute-start(f32[2,32,128]{2,1,0:T(8,128)S(1)} %fusion.2), channel_id=1, source_target_pairs={{0,32},{16,48},{32,0},{48,16},{64,96},{80,112},{96,64},{112,80},{1... | collective-permute-start | bytes 98312 | tf_op jit(solution)/shard_map/ppermute | solution.py:270
  34.7 5.2 %collective-permute-start.7 = (f32[32,8,128]{2,0,1:T(8,128)S(1)}, f32[32,8,128]{2,0,1:T(8,128)S(1)}, u32[]{:S(2)}, u32[]{:S(2)}) collective-permute-start(f32[32,8,128]{2,0,1:T(8,128)S(1)} %add.36), channel_id=1, source_target_pairs={{0,32},{16,112},{32,0},{48,80},{64,96},{80,48},{96,64},{112,16},{1... | collective-permute-start | bytes 393224 | tf_op jit(solution)/shard_map/ppermute | solution.py:270
  39.9 3.6 %collective-permute-start.8 = (f32[32,8,128]{2,0,1:T(8,128)S(1)}, f32[32,8,128]{2,0,1:T(8,128)S(1)}, u32[]{:S(2)}, u32[]{:S(2)}) collective-permute-start(f32[32,8,128]{2,0,1:T(8,128)S(1)} %add.37), channel_id=1, source_target_pairs={{0,16},{16,0},{32,48},{48,32},{64,80},{80,64},{96,112},{112,96},{1... | collective-permute-start | bytes 393224 | tf_op jit(solution)/shard_map/ppermute | solution.py:270

commit v3 on v2

--- a/solution.py
+++ b/solution.py
@@ -293,9 +293,10 @@
     even_rim = exchange(jnp.where(odd, first, last), band, lambda i: i ^ 1)
     odd_rim = exchange(jnp.where(odd, last, first), band, lambda i: (i + (1 if i % 2 else -1)) % count)
     rim = jnp.stack([jnp.where(odd, even_rim, odd_rim), jnp.where(odd, odd_rim, even_rim)])
-    rim_sum = rim
-    for cross in (1, 6, 2):
-        rim_sum = rim_sum + exchange(rim_sum, "coarse", lambda i: i ^ cross)
+    pair = rim + exchange(rim, "coarse", lambda i: i ^ 1)
+    rim_sum = pair
+    for cross in (2, 6, 4):
+        rim_sum = rim_sum + exchange(pair, "coarse", lambda i: i ^ cross)
     inside_band = jnp.stack([place > 0, place < count - 1])[:, None, None]
     rim = jnp.where(inside_band, rim * (1.0 / (rim_sum / channels)) - 1.0, 0.0)
 

time: 49.2 us -> 47.9 us (0.974)
  waiting for transfers between devices: 10.3 us -> 6.23 us
  starting transfers between devices: 31.8 us -> 34.6 us
    ppermute x9 -> x10, waiting for transfers between devices: 10.3 us -> 6.23 us  [exchange(): lax.ppermute(value, axes, [(i, j) for i, j in pairs if j is not None])]
    ppermute x9 -> x10, starting transfers between devices: 31.8 us -> 34.6 us  [exchange(): lax.ppermute(value, axes, [(i, j) for i, j in pairs if j is not None])]
  transfers between devices with their start and end apart: 9 -> 10, of which waited for: 7 -> 6; matrix products, arithmetic and copies ran while one was open for 0% -> 0% of each run, Pallas kernels for 0% -> 0%
where the time goes in v3:
time: 47.9 us; the launch traced here: 47.8 us
  starting transfers between devices  34.6 us (72%)
  waiting for transfers between devices  6.23 us (13%)
  Pallas kernels  5.38 us (11%)
  local copies, waits for them, and re-layouts  1.2 us (3%)
    ppermute x10, starting transfers between devices, exchange(): lax.ppermute(value, axes, [(i, j) for i, j in pairs if j is not None])  34.6 us
    ppermute x10, waiting for transfers between devices, exchange(): lax.ppermute(value, axes, [(i, j) for i, j in pairs if j is not None])  6.23 us
    pallas_call x1, Pallas kernels, call(): pl.pallas_call(kernel, out_shape=jax.ShapeDtypeStruct((paths, chunks, LAN...  3.33 us
    pallas_call x1, Pallas kernels, call(): pl.pallas_call(kernel, out_shape=(shape, shape), in_specs=[pl.BlockSpec(m...  2.05 us
    slice x1, local copies, waits for them, and re-layouts, search(): x[:, half:]  1.03 us
  transfers between devices with their start and end apart: 10, of which 6 were waited for; matrix products, arithmetic and copies ran while one was open for 0% of the time, Pallas kernels for 0%

profile of v3, /device:TPU:33, one launch (start us, length us, event | category | flops | bytes accessed | tf_op | source)
XLA Modules:
  0.0 47.8 jit_solution(11954126196954043781)
XLA Ops:
  0.0 0.0 copy-start
  0.0 1.0 %fusion.1 = (f32[32,8,128]{2,1,0:T(8,128)S(1)}, f32[32,8,128]{2,1,0:T(8,128)S(1)}) fusion(f32[32,16,128]{2,1,0:T(8,128)} %bitcast.17), kind=kLoop, calls=%fused_computation.16 | loop fusion | bytes 524288 | tf_op jit(solution)/shard_map/slice | solution.py:285
  1.1 3.4 %collective-permute-start = (f32[32,128]{1,0:T(8,128)S(1)}, f32[32,128]{1,0:T(8,128)S(1)}, u32[]{:S(2)}, u32[]{:S(2)}) collective-permute-start(f32[32,128]{1,0:T(8,128)S(1)} %get-tuple-element.13), channel_id=1, source_target_pairs={{0,1},{1,0},{2,3},{3,2},{4,5},{5,4},{6,7},{7,6},{8,9},{9,8},{10,11... | collective-permute-start | bytes 49160 | tf_op jit(solution)/shard_map/ppermute | solution.py:270
  4.5 20.2 %collective-permute-start.1 = (f32[32,128]{1,0:T(8,128)S(1)}, f32[32,128]{1,0:T(8,128)S(1)}, u32[]{:S(2)}, u32[]{:S(2)}) collective-permute-start(f32[32,128]{1,0:T(8,128)S(1)} %get-tuple-element.14), channel_id=1, source_target_pairs={{0,127},{1,2},{2,1},{3,4},{4,3},{5,6},{6,5},{7,8},{8,7},{9,10},{10... | collective-permute-start | bytes 49160 | tf_op jit(solution)/shard_map/ppermute | solution.py:270
  24.8 2.5 %collective-permute-start.6 = (f32[32,8,128]{2,0,1:T(8,128)S(1)}, f32[32,8,128]{2,0,1:T(8,128)S(1)}, u32[]{:S(2)}, u32[]{:S(2)}) collective-permute-start(f32[32,8,128]{2,0,1:T(8,128)S(1)} %get-tuple-element.8), channel_id=1, source_target_pairs={{0,16},{16,0},{32,48},{48,32},{64,80},{80,64},{96,112},{112,96},{1... | collective-permute-start | bytes 393224 | tf_op jit(solution)/shard_map/ppermute | solution.py:270
  27.3 0.0 collective-permute-done
  27.3 0.0 collective-permute-done.1
  27.3 1.6 %collective-permute-start.2 = (f32[2,32,128]{2,1,0:T(8,128)S(1)}, f32[2,32,128]{2,1,0:T(8,128)S(1)}, u32[]{:S(2)}, u32[]{:S(2)}) collective-permute-start(f32[2,32,128]{2,1,0:T(8,128)S(1)} %pad_maximum_fusion), channel_id=1, source_target_pairs={{0,16},{16,0},{32,48},{48,32},{64,80},{80,64},{96,112},{112,96},{1... | collective-permute-start | bytes 98312 | tf_op jit(solution)/shard_map/ppermute | solution.py:270
  28.9 0.0 collective-permute-done.6
  28.9 0.1 collective-permute-start.7
  29.0 0.7 %collective-permute-done.2 = f32[2,32,128]{2,1,0:T(8,128)S(1)} collective-permute-done((f32[2,32,128]{2,1,0:T(8,128)S(1)}, f32[2,32,128]{2,1,0:T(8,128)S(1)}, u32[]{:S(2)}, u32[]{:S(2)}) %collective-permute-start.2) | collective-permute-done | bytes 32800 | tf_op jit(solution)/shard_map/ppermute | solution.py:270
  29.7 0.7 %collective-permute-start.4 = (f32[2,32,128]{2,1,0:T(8,128)S(1)}, f32[2,32,128]{2,1,0:T(8,128)S(1)}, u32[]{:S(2)}, u32[]{:S(2)}) collective-permute-start(f32[2,32,128]{2,1,0:T(8,128)S(1)} %fusion), channel_id=1, source_target_pairs={{0,96},{16,112},{32,64},{48,80},{64,32},{80,48},{96,0},{112,16},{1... | collective-permute-start | bytes 98312 | tf_op jit(solution)/shard_map/ppermute | solution.py:270
  30.5 1.9 %collective-permute-start.5 = (f32[2,32,128]{2,1,0:T(8,128)S(1)}, f32[2,32,128]{2,1,0:T(8,128)S(1)}, u32[]{:S(2)}, u32[]{:S(2)}) collective-permute-start(f32[2,32,128]{2,1,0:T(8,128)S(1)} %fusion), channel_id=1, source_target_pairs={{0,64},{16,80},{32,96},{48,112},{64,0},{80,16},{96,32},{112,48},{1... | collective-permute-start | bytes 98312 | tf_op jit(solution)/shard_map/ppermute | solution.py:270
  32.4 0.6 %collective-permute-start.3 = (f32[2,32,128]{2,1,0:T(8,128)S(1)}, f32[2,32,128]{2,1,0:T(8,128)S(1)}, u32[]{:S(2)}, u32[]{:S(2)}) collective-permute-start(f32[2,32,128]{2,1,0:T(8,128)S(1)} %fusion), channel_id=1, source_target_pairs={{0,32},{16,48},{32,0},{48,16},{64,96},{80,112},{96,64},{112,80},{1... | collective-permute-start | bytes 98312 | tf_op jit(solution)/shard_map/ppermute | solution.py:270
  33.0 0.1 pad_add_fusion
  33.1 0.0 collective-permute-done.7
  33.1 0.8 %collective-permute-start.8 = (f32[32,8,128]{2,0,1:T(8,128)S(1)}, f32[32,8,128]{2,0,1:T(8,128)S(1)}, u32[]{:S(2)}, u32[]{:S(2)}) collective-permute-start(f32[32,8,128]{2,0,1:T(8,128)S(1)} %add.40), channel_id=1, source_target_pairs={{0,32},{16,112},{32,0},{48,80},{64,96},{80,48},{96,64},{112,16},{1... | collective-permute-start | bytes 393224 | tf_op jit(solution)/shard_map/ppermute | solution.py:270
  33.9 0.4 collective-permute-done.4
  34.4 0.5 %collective-permute-done.5 = f32[2,32,128]{2,1,0:T(8,128)S(1)} collective-permute-done((f32[2,32,128]{2,1,0:T(8,128)S(1)}, f32[2,32,128]{2,1,0:T(8,128)S(1)}, u32[]{:S(2)}, u32[]{:S(2)}) %collective-permute-start.5) | collective-permute-done | bytes 32800 | tf_op jit(solution)/shard_map/ppermute | solution.py:270
  34.8 0.6 %collective-permute-done.3 = f32[2,32,128]{2,1,0:T(8,128)S(1)} collective-permute-done((f32[2,32,128]{2,1,0:T(8,128)S(1)}, f32[2,32,128]{2,1,0:T(8,128)S(1)}, u32[]{:S(2)}, u32[]{:S(2)}) %collective-permute-start.3) | collective-permute-done | bytes 32800 | tf_op jit(solution)/shard_map/ppermute | solution.py:270
  35.5 0.1 add_select_fusion
  35.5 3.0 %collective-permute-done.8 = f32[32,8,128]{2,0,1:T(8,128)S(1)} collective-permute-done((f32[32,8,128]{2,0,1:T(8,128)S(1)}, f32[32,8,128]{2,0,1:T(8,128)S(1)}, u32[]{:S(2)}, u32[]{:S(2)}) %collective-permute-start.8) | collective-permute-done | bytes 131104 | tf_op jit(solution)/shard_map/ppermute | solution.py:270
  38.6 2.6 %collective-permute-start.9 = (f32[32,8,128]{2,0,1:T(8,128)S(1)}, f32[32,8,128]{2,0,1:T(8,128)S(1)}, u32[]{:S(2)}, u32[]{:S(2)}) collective-permute-start(f32[32,8,128]{2,0,1:T(8,128)S(1)} %add.41), channel_id=1, source_target_pairs={{0,16},{16,0},{32,48},{48,32},{64,80},{80,64},{96,112},{112,96},{1... | collective-permute-start | bytes 393224 | tf_op jit(solution)/shard_map/ppermute | solution.py:270
  41.2 1.0 %collective-permute-done.9 = f32[32,8,128]{2,0,1:T(8,128)S(1)} collective-permute-done((f32[32,8,128]{2,0,1:T(8,128)S(1)}, f32[32,8,128]{2,0,1:T(8,128)S(1)}, u32[]{:S(2)}, u32[]{:S(2)}) %collective-permute-start.9) | collective-permute-done | bytes 131104 | tf_op jit(solution)/shard_map/ppermute | solution.py:270
  42.2 0.1 copy.10.high_ref
  42.3 0.1 copy.9.low_ref
  42.4 0.0 copy-done
  42.4 3.3 %inside.1.stage_ref = f32[256,16,128]{2,1,0:T(8,128)S(1)} custom-call(f32[32,16,128]{2,1,0:T(8,128)S(1)} %bitcast.18, f32[32,8,128]{2,1,0:T(8,128)S(1)} %copy.9.low_ref, f32[32,8,128]{2,1,0:T(8,128)S(1)} %copy.10.high_ref, s32[1]{0:T(128)} %bitcast.9.end_ref), custom_call_target="tpu_custom_call" | custom-call | flops 40000000 | bytes 2097152 | tf_op jit(solution)/shard_map/inside/pallas_call | solution.py:159
  45.7 2.1 %edges.1 = (f32[256,16,128]{2,1,0:T(8,128)S(1)}, f32[256,16,128]{2,1,0:T(8,128)}) custom-call(f32[32,128]{1,0:T(8,128)S(1)} %get-tuple-element.20.lo_ref, f32[32,128]{1,0:T(8,128)S(1)} %get-tuple-element.19.hi_ref, f32[256,16,128]{2,1,0:T(8,128)S(1)} %inside.1.stage_ref), custom_call_target="tpu_custom_call", output_to_operand_aliasing={{0}: (2, {})} | custom-call | tf_op jit(solution)/shard_map/edges/pallas_call | solution.py:251
  (10 shorter events, 0.2 us)
Async XLA Ops:
  0.0 42.4 %copy-start = (f32[32,1,2048]{2,1,0:T(1,128)S(1)}, f32[32,1,2048]{2,1,0:T(1,128)}, u32[]{:S(2)}) copy-start(f32[32,1,2048]{2,1,0:T(1,128)} %param.1) | copy-start | bytes 786436
  1.1 26.2 %collective-permute-start = (f32[32,128]{1,0:T(8,128)S(1)}, f32[32,128]{1,0:T(8,128)S(1)}, u32[]{:S(2)}, u32[]{:S(2)}) collective-permute-start(f32[32,128]{1,0:T(8,128)S(1)} %get-tuple-element.13), channel_id=1, source_target_pairs={{0,1},{1,0},{2,3},{3,2},{4,5},{5,4},{6,7},{7,6},{8,9},{9,8},{10,11... | collective-permute-start | bytes 49160 | tf_op jit(solution)/shard_map/ppermute | solution.py:270
  4.5 22.8 %collective-permute-start.1 = (f32[32,128]{1,0:T(8,128)S(1)}, f32[32,128]{1,0:T(8,128)S(1)}, u32[]{:S(2)}, u32[]{:S(2)}) collective-permute-start(f32[32,128]{1,0:T(8,128)S(1)} %get-tuple-element.14), channel_id=1, source_target_pairs={{0,127},{1,2},{2,1},{3,4},{4,3},{5,6},{6,5},{7,8},{8,7},{9,10},{10... | collective-permute-start | bytes 49160 | tf_op jit(solution)/shard_map/ppermute | solution.py:270
  24.8 4.1 %collective-permute-start.6 = (f32[32,8,128]{2,0,1:T(8,128)S(1)}, f32[32,8,128]{2,0,1:T(8,128)S(1)}, u32[]{:S(2)}, u32[]{:S(2)}) collective-permute-start(f32[32,8,128]{2,0,1:T(8,128)S(1)} %get-tuple-element.8), channel_id=1, source_target_pairs={{0,16},{16,0},{32,48},{48,32},{64,80},{80,64},{96,112},{112,96},{1... | collective-permute-start | bytes 393224 | tf_op jit(solution)/shard_map/ppermute | solution.py:270
  27.3 2.4 %collective-permute-start.2 = (f32[2,32,128]{2,1,0:T(8,128)S(1)}, f32[2,32,128]{2,1,0:T(8,128)S(1)}, u32[]{:S(2)}, u32[]{:S(2)}) collective-permute-start(f32[2,32,128]{2,1,0:T(8,128)S(1)} %pad_maximum_fusion), channel_id=1, source_target_pairs={{0,16},{16,0},{32,48},{48,32},{64,80},{80,64},{96,112},{112,96},{1... | collective-permute-start | bytes 98312 | tf_op jit(solution)/shard_map/ppermute | solution.py:270
  28.9 4.2 %collective-permute-start.7 = (f32[32,8,128]{2,0,1:T(8,128)S(1)}, f32[32,8,128]{2,0,1:T(8,128)S(1)}, u32[]{:S(2)}, u32[]{:S(2)}) collective-permute-start(f32[32,8,128]{2,0,1:T(8,128)S(1)} %add.39), channel_id=1, source_target_pairs={{0,96},{16,48},{32,64},{48,16},{64,32},{80,112},{96,0},{112,80},{1... | collective-permute-start | bytes 393224 | tf_op jit(solution)/shard_map/ppermute | solution.py:270
  29.7 4.6 %collective-permute-start.4 = (f32[2,32,128]{2,1,0:T(8,128)S(1)}, f32[2,32,128]{2,1,0:T(8,128)S(1)}, u32[]{:S(2)}, u32[]{:S(2)}) collective-permute-start(f32[2,32,128]{2,1,0:T(8,128)S(1)} %fusion), channel_id=1, source_target_pairs={{0,96},{16,112},{32,64},{48,80},{64,32},{80,48},{96,0},{112,16},{1... | collective-permute-start | bytes 98312 | tf_op jit(solution)/shard_map/ppermute | solution.py:270
  30.5 4.4 %collective-permute-start.5 = (f32[2,32,128]{2,1,0:T(8,128)S(1)}, f32[2,32,128]{2,1,0:T(8,128)S(1)}, u32[]{:S(2)}, u32[]{:S(2)}) collective-permute-start(f32[2,32,128]{2,1,0:T(8,128)S(1)} %fusion), channel_id=1, source_target_pairs={{0,64},{16,80},{32,96},{48,112},{64,0},{80,16},{96,32},{112,48},{1... | collective-permute-start | bytes 98312 | tf_op jit(solution)/shard_map/ppermute | solution.py:270
  32.4 3.1 %collective-permute-start.3 = (f32[2,32,128]{2,1,0:T(8,128)S(1)}, f32[2,32,128]{2,1,0:T(8,128)S(1)}, u32[]{:S(2)}, u32[]{:S(2)}) collective-permute-start(f32[2,32,128]{2,1,0:T(8,128)S(1)} %fusion), channel_id=1, source_target_pairs={{0,32},{16,48},{32,0},{48,16},{64,96},{80,112},{96,64},{112,80},{1... | collective-permute-start | bytes 98312 | tf_op jit(solution)/shard_map/ppermute | solution.py:270
  33.1 5.5 %collective-permute-start.8 = (f32[32,8,128]{2,0,1:T(8,128)S(1)}, f32[32,8,128]{2,0,1:T(8,128)S(1)}, u32[]{:S(2)}, u32[]{:S(2)}) collective-permute-start(f32[32,8,128]{2,0,1:T(8,128)S(1)} %add.40), channel_id=1, source_target_pairs={{0,32},{16,112},{32,0},{48,80},{64,96},{80,48},{96,64},{112,16},{1... | collective-permute-start | bytes 393224 | tf_op jit(solution)/shard_map/ppermute | solution.py:270
  38.6 3.6 %collective-permute-start.9 = (f32[32,8,128]{2,0,1:T(8,128)S(1)}, f32[32,8,128]{2,0,1:T(8,128)S(1)}, u32[]{:S(2)}, u32[]{:S(2)}) collective-permute-start(f32[32,8,128]{2,0,1:T(8,128)S(1)} %add.41), channel_id=1, source_target_pairs={{0,16},{16,0},{32,48},{48,32},{64,80},{80,64},{96,112},{112,96},{1... | collective-permute-start | bytes 393224 | tf_op jit(solution)/shard_map/ppermute | solution.py:270

commit v4 on v3

--- a/solution.py
+++ b/solution.py
@@ -297,8 +297,9 @@
     rim_sum = pair
     for cross in (2, 6, 4):
         rim_sum = rim_sum + exchange(pair, "coarse", lambda i: i ^ cross)
-    inside_band = jnp.stack([place > 0, place < count - 1])[:, None, None]
-    rim = jnp.where(inside_band, rim * (1.0 / (rim_sum / channels)) - 1.0, 0.0)
+    rim = rim * (1.0 / (rim_sum / channels)) - 1.0
+    before = jnp.where(place > 0, rim[0], 0.0)
+    after = jnp.where(place < count - 1, rim[1], 0.0)
 
     for near, far in ((6, 2), (2, 6)):
         total = total + exchange(total, "coarse", lambda i: i ^ (far if i % 2 else near))
@@ -306,7 +307,7 @@
     low, high = jnp.where(upper, other, total), jnp.where(upper, total, other)
     at_end = (place == count - 1).astype(jnp.int32).reshape(1)
     stage = inside(rows, chunks, channels)(x, low, high, at_end)
-    out = edges(rows, chunks)(rim[0], rim[1], stage)
+    out = edges(rows, chunks)(before, after, stage)
     return out.reshape(RATES, rows, 1, columns)
 
 

time: 47.9 us -> 47.9 us (level)
  no operation moved by 1% of the time
where the time goes in v4:
time: 47.9 us; the launch traced here: 47.8 us
  starting transfers between devices  34.6 us (72%)
  waiting for transfers between devices  6.31 us (13%)
  Pallas kernels  5.38 us (11%)
  local copies, waits for them, and re-layouts  1.2 us (3%)
    ppermute x10, starting transfers between devices, exchange(): lax.ppermute(value, axes, [(i, j) for i, j in pairs if j is not None])  34.6 us
    ppermute x10, waiting for transfers between devices, exchange(): lax.ppermute(value, axes, [(i, j) for i, j in pairs if j is not None])  6.31 us
    pallas_call x1, Pallas kernels, call(): pl.pallas_call(kernel, out_shape=jax.ShapeDtypeStruct((paths, chunks, LAN...  3.33 us
    pallas_call x1, Pallas kernels, call(): pl.pallas_call(kernel, out_shape=(shape, shape), in_specs=[pl.BlockSpec(m...  2.05 us
    slice x1, local copies, waits for them, and re-layouts, search(): x[:, half:]  1.03 us
  transfers between devices with their start and end apart: 10, of which 6 were waited for; matrix products, arithmetic and copies ran while one was open for 0% of the time, Pallas kernels for 0%

profile of v4, /device:TPU:33, one launch (start us, length us, event | category | flops | bytes accessed | tf_op | source)
XLA Modules:
  0.0 47.8 jit_solution(5395648016934238628)
XLA Ops:
  0.0 0.0 copy-start
  0.0 1.0 %fusion.3 = (f32[32,8,128]{2,1,0:T(8,128)S(1)}, f32[32,8,128]{2,1,0:T(8,128)S(1)}) fusion(f32[32,16,128]{2,1,0:T(8,128)} %bitcast.15), kind=kLoop, calls=%fused_computation.17 | loop fusion | bytes 524288 | tf_op jit(solution)/shard_map/slice | solution.py:285
  1.1 3.4 %collective-permute-start = (f32[32,128]{1,0:T(8,128)S(1)}, f32[32,128]{1,0:T(8,128)S(1)}, u32[]{:S(2)}, u32[]{:S(2)}) collective-permute-start(f32[32,128]{1,0:T(8,128)S(1)} %get-tuple-element.13), channel_id=1, source_target_pairs={{0,1},{1,0},{2,3},{3,2},{4,5},{5,4},{6,7},{7,6},{8,9},{9,8},{10,11... | collective-permute-start | bytes 49160 | tf_op jit(solution)/shard_map/ppermute | solution.py:270
  4.5 20.2 %collective-permute-start.1 = (f32[32,128]{1,0:T(8,128)S(1)}, f32[32,128]{1,0:T(8,128)S(1)}, u32[]{:S(2)}, u32[]{:S(2)}) collective-permute-start(f32[32,128]{1,0:T(8,128)S(1)} %get-tuple-element.14), channel_id=1, source_target_pairs={{0,127},{1,2},{2,1},{3,4},{4,3},{5,6},{6,5},{7,8},{8,7},{9,10},{10... | collective-permute-start | bytes 49160 | tf_op jit(solution)/shard_map/ppermute | solution.py:270
  24.8 2.5 %collective-permute-start.6 = (f32[32,8,128]{2,0,1:T(8,128)S(1)}, f32[32,8,128]{2,0,1:T(8,128)S(1)}, u32[]{:S(2)}, u32[]{:S(2)}) collective-permute-start(f32[32,8,128]{2,0,1:T(8,128)S(1)} %get-tuple-element.8), channel_id=1, source_target_pairs={{0,16},{16,0},{32,48},{48,32},{64,80},{80,64},{96,112},{112,96},{1... | collective-permute-start | bytes 393224 | tf_op jit(solution)/shard_map/ppermute | solution.py:270
  27.3 0.0 collective-permute-done
  27.3 0.0 collective-permute-done.1
  27.3 1.6 %collective-permute-start.2 = (f32[2,32,128]{2,1,0:T(8,128)S(1)}, f32[2,32,128]{2,1,0:T(8,128)S(1)}, u32[]{:S(2)}, u32[]{:S(2)}) collective-permute-start(f32[2,32,128]{2,1,0:T(8,128)S(1)} %pad_maximum_fusion), channel_id=1, source_target_pairs={{0,16},{16,0},{32,48},{48,32},{64,80},{80,64},{96,112},{112,96},{1... | collective-permute-start | bytes 98312 | tf_op jit(solution)/shard_map/ppermute | solution.py:270
  28.9 0.0 collective-permute-done.6
  28.9 0.1 collective-permute-start.7
  29.0 0.7 %collective-permute-done.2 = f32[2,32,128]{2,1,0:T(8,128)S(1)} collective-permute-done((f32[2,32,128]{2,1,0:T(8,128)S(1)}, f32[2,32,128]{2,1,0:T(8,128)S(1)}, u32[]{:S(2)}, u32[]{:S(2)}) %collective-permute-start.2) | collective-permute-done | bytes 32800 | tf_op jit(solution)/shard_map/ppermute | solution.py:270
  29.7 0.7 %collective-permute-start.4 = (f32[2,32,128]{2,1,0:T(8,128)S(1)}, f32[2,32,128]{2,1,0:T(8,128)S(1)}, u32[]{:S(2)}, u32[]{:S(2)}) collective-permute-start(f32[2,32,128]{2,1,0:T(8,128)S(1)} %fusion.2), channel_id=1, source_target_pairs={{0,96},{16,112},{32,64},{48,80},{64,32},{80,48},{96,0},{112,16},{1... | collective-permute-start | bytes 98312 | tf_op jit(solution)/shard_map/ppermute | solution.py:270
  30.5 1.9 %collective-permute-start.5 = (f32[2,32,128]{2,1,0:T(8,128)S(1)}, f32[2,32,128]{2,1,0:T(8,128)S(1)}, u32[]{:S(2)}, u32[]{:S(2)}) collective-permute-start(f32[2,32,128]{2,1,0:T(8,128)S(1)} %fusion.2), channel_id=1, source_target_pairs={{0,64},{16,80},{32,96},{48,112},{64,0},{80,16},{96,32},{112,48},{1... | collective-permute-start | bytes 98312 | tf_op jit(solution)/shard_map/ppermute | solution.py:270
  32.4 0.6 %collective-permute-start.3 = (f32[2,32,128]{2,1,0:T(8,128)S(1)}, f32[2,32,128]{2,1,0:T(8,128)S(1)}, u32[]{:S(2)}, u32[]{:S(2)}) collective-permute-start(f32[2,32,128]{2,1,0:T(8,128)S(1)} %fusion.2), channel_id=1, source_target_pairs={{0,32},{16,48},{32,0},{48,16},{64,96},{80,112},{96,64},{112,80},{1... | collective-permute-start | bytes 98312 | tf_op jit(solution)/shard_map/ppermute | solution.py:270
  33.0 0.0 collective-permute-done.7
  33.0 0.8 %collective-permute-start.8 = (f32[32,8,128]{2,0,1:T(8,128)S(1)}, f32[32,8,128]{2,0,1:T(8,128)S(1)}, u32[]{:S(2)}, u32[]{:S(2)}) collective-permute-start(f32[32,8,128]{2,0,1:T(8,128)S(1)} %add.40), channel_id=1, source_target_pairs={{0,32},{16,112},{32,0},{48,80},{64,96},{80,48},{96,64},{112,16},{1... | collective-permute-start | bytes 393224 | tf_op jit(solution)/shard_map/ppermute | solution.py:270
  33.9 0.5 %collective-permute-done.4 = f32[2,32,128]{2,1,0:T(8,128)S(1)} collective-permute-done((f32[2,32,128]{2,1,0:T(8,128)S(1)}, f32[2,32,128]{2,1,0:T(8,128)S(1)}, u32[]{:S(2)}, u32[]{:S(2)}) %collective-permute-start.4) | collective-permute-done | bytes 32800 | tf_op jit(solution)/shard_map/ppermute | solution.py:270
  34.4 0.5 collective-permute-done.5
  34.8 0.6 %collective-permute-done.3 = f32[2,32,128]{2,1,0:T(8,128)S(1)} collective-permute-done((f32[2,32,128]{2,1,0:T(8,128)S(1)}, f32[2,32,128]{2,1,0:T(8,128)S(1)}, u32[]{:S(2)}, u32[]{:S(2)}) %collective-permute-start.3) | collective-permute-done | bytes 32800 | tf_op jit(solution)/shard_map/ppermute | solution.py:270
  35.5 3.0 %collective-permute-done.8 = f32[32,8,128]{2,0,1:T(8,128)S(1)} collective-permute-done((f32[32,8,128]{2,0,1:T(8,128)S(1)}, f32[32,8,128]{2,0,1:T(8,128)S(1)}, u32[]{:S(2)}, u32[]{:S(2)}) %collective-permute-start.8) | collective-permute-done | bytes 131104 | tf_op jit(solution)/shard_map/ppermute | solution.py:270
  38.5 2.7 %collective-permute-start.9 = (f32[32,8,128]{2,0,1:T(8,128)S(1)}, f32[32,8,128]{2,0,1:T(8,128)S(1)}, u32[]{:S(2)}, u32[]{:S(2)}) collective-permute-start(f32[32,8,128]{2,0,1:T(8,128)S(1)} %add.41), channel_id=1, source_target_pairs={{0,16},{16,0},{32,48},{48,32},{64,80},{80,64},{96,112},{112,96},{1... | collective-permute-start | bytes 393224 | tf_op jit(solution)/shard_map/ppermute | solution.py:270
  41.2 1.0 %collective-permute-done.9 = f32[32,8,128]{2,0,1:T(8,128)S(1)} collective-permute-done((f32[32,8,128]{2,0,1:T(8,128)S(1)}, f32[32,8,128]{2,0,1:T(8,128)S(1)}, u32[]{:S(2)}, u32[]{:S(2)}) %collective-permute-start.9) | collective-permute-done | bytes 131104 | tf_op jit(solution)/shard_map/ppermute | solution.py:270
  42.2 0.1 copy.10.high_ref
  42.3 0.1 copy.9.low_ref
  42.4 0.0 copy-done
  42.4 3.3 %inside.1.stage_ref = f32[256,16,128]{2,1,0:T(8,128)S(1)} custom-call(f32[32,16,128]{2,1,0:T(8,128)S(1)} %bitcast.16, f32[32,8,128]{2,1,0:T(8,128)S(1)} %copy.9.low_ref, f32[32,8,128]{2,1,0:T(8,128)S(1)} %copy.10.high_ref, s32[1]{0:T(128)} %bitcast.7.end_ref), custom_call_target="tpu_custom_call" | custom-call | flops 40000000 | bytes 2097152 | tf_op jit(solution)/shard_map/inside/pallas_call | solution.py:159
  45.7 2.1 %edges.1 = (f32[256,16,128]{2,1,0:T(8,128)S(1)}, f32[256,16,128]{2,1,0:T(8,128)}) custom-call(f32[32,128]{1,0:T(8,128)S(1)} %get-tuple-element.20.lo_ref, f32[32,128]{1,0:T(8,128)S(1)} %get-tuple-element.19.hi_ref, f32[256,16,128]{2,1,0:T(8,128)S(1)} %inside.1.stage_ref), custom_call_target="tpu_custom_call", output_to_operand_aliasing={{0}: (2, {})} | custom-call | tf_op jit(solution)/shard_map/edges/pallas_call | solution.py:251
  (11 shorter events, 0.2 us)
Async XLA Ops:
  0.0 42.4 %copy-start = (f32[32,1,2048]{2,1,0:T(1,128)S(1)}, f32[32,1,2048]{2,1,0:T(1,128)}, u32[]{:S(2)}) copy-start(f32[32,1,2048]{2,1,0:T(1,128)} %param.1) | copy-start | bytes 786436
  1.1 26.2 %collective-permute-start = (f32[32,128]{1,0:T(8,128)S(1)}, f32[32,128]{1,0:T(8,128)S(1)}, u32[]{:S(2)}, u32[]{:S(2)}) collective-permute-start(f32[32,128]{1,0:T(8,128)S(1)} %get-tuple-element.13), channel_id=1, source_target_pairs={{0,1},{1,0},{2,3},{3,2},{4,5},{5,4},{6,7},{7,6},{8,9},{9,8},{10,11... | collective-permute-start | bytes 49160 | tf_op jit(solution)/shard_map/ppermute | solution.py:270
  4.5 22.8 %collective-permute-start.1 = (f32[32,128]{1,0:T(8,128)S(1)}, f32[32,128]{1,0:T(8,128)S(1)}, u32[]{:S(2)}, u32[]{:S(2)}) collective-permute-start(f32[32,128]{1,0:T(8,128)S(1)} %get-tuple-element.14), channel_id=1, source_target_pairs={{0,127},{1,2},{2,1},{3,4},{4,3},{5,6},{6,5},{7,8},{8,7},{9,10},{10... | collective-permute-start | bytes 49160 | tf_op jit(solution)/shard_map/ppermute | solution.py:270
  24.8 4.1 %collective-permute-start.6 = (f32[32,8,128]{2,0,1:T(8,128)S(1)}, f32[32,8,128]{2,0,1:T(8,128)S(1)}, u32[]{:S(2)}, u32[]{:S(2)}) collective-permute-start(f32[32,8,128]{2,0,1:T(8,128)S(1)} %get-tuple-element.8), channel_id=1, source_target_pairs={{0,16},{16,0},{32,48},{48,32},{64,80},{80,64},{96,112},{112,96},{1... | collective-permute-start | bytes 393224 | tf_op jit(solution)/shard_map/ppermute | solution.py:270
  27.3 2.4 %collective-permute-start.2 = (f32[2,32,128]{2,1,0:T(8,128)S(1)}, f32[2,32,128]{2,1,0:T(8,128)S(1)}, u32[]{:S(2)}, u32[]{:S(2)}) collective-permute-start(f32[2,32,128]{2,1,0:T(8,128)S(1)} %pad_maximum_fusion), channel_id=1, source_target_pairs={{0,16},{16,0},{32,48},{48,32},{64,80},{80,64},{96,112},{112,96},{1... | collective-permute-start | bytes 98312 | tf_op jit(solution)/shard_map/ppermute | solution.py:270
  28.9 4.1 %collective-permute-start.7 = (f32[32,8,128]{2,0,1:T(8,128)S(1)}, f32[32,8,128]{2,0,1:T(8,128)S(1)}, u32[]{:S(2)}, u32[]{:S(2)}) collective-permute-start(f32[32,8,128]{2,0,1:T(8,128)S(1)} %add.39), channel_id=1, source_target_pairs={{0,96},{16,48},{32,64},{48,16},{64,32},{80,112},{96,0},{112,80},{1... | collective-permute-start | bytes 393224 | tf_op jit(solution)/shard_map/ppermute | solution.py:270
  29.7 4.6 %collective-permute-start.4 = (f32[2,32,128]{2,1,0:T(8,128)S(1)}, f32[2,32,128]{2,1,0:T(8,128)S(1)}, u32[]{:S(2)}, u32[]{:S(2)}) collective-permute-start(f32[2,32,128]{2,1,0:T(8,128)S(1)} %fusion.2), channel_id=1, source_target_pairs={{0,96},{16,112},{32,64},{48,80},{64,32},{80,48},{96,0},{112,16},{1... | collective-permute-start | bytes 98312 | tf_op jit(solution)/shard_map/ppermute | solution.py:270
  30.5 4.4 %collective-permute-start.5 = (f32[2,32,128]{2,1,0:T(8,128)S(1)}, f32[2,32,128]{2,1,0:T(8,128)S(1)}, u32[]{:S(2)}, u32[]{:S(2)}) collective-permute-start(f32[2,32,128]{2,1,0:T(8,128)S(1)} %fusion.2), channel_id=1, source_target_pairs={{0,64},{16,80},{32,96},{48,112},{64,0},{80,16},{96,32},{112,48},{1... | collective-permute-start | bytes 98312 | tf_op jit(solution)/shard_map/ppermute | solution.py:270
  32.4 3.1 %collective-permute-start.3 = (f32[2,32,128]{2,1,0:T(8,128)S(1)}, f32[2,32,128]{2,1,0:T(8,128)S(1)}, u32[]{:S(2)}, u32[]{:S(2)}) collective-permute-start(f32[2,32,128]{2,1,0:T(8,128)S(1)} %fusion.2), channel_id=1, source_target_pairs={{0,32},{16,48},{32,0},{48,16},{64,96},{80,112},{96,64},{112,80},{1... | collective-permute-start | bytes 98312 | tf_op jit(solution)/shard_map/ppermute | solution.py:270
  33.0 5.5 %collective-permute-start.8 = (f32[32,8,128]{2,0,1:T(8,128)S(1)}, f32[32,8,128]{2,0,1:T(8,128)S(1)}, u32[]{:S(2)}, u32[]{:S(2)}) collective-permute-start(f32[32,8,128]{2,0,1:T(8,128)S(1)} %add.40), channel_id=1, source_target_pairs={{0,32},{16,112},{32,0},{48,80},{64,96},{80,48},{96,64},{112,16},{1... | collective-permute-start | bytes 393224 | tf_op jit(solution)/shard_map/ppermute | solution.py:270
  38.5 3.6 %collective-permute-start.9 = (f32[32,8,128]{2,0,1:T(8,128)S(1)}, f32[32,8,128]{2,0,1:T(8,128)S(1)}, u32[]{:S(2)}, u32[]{:S(2)}) collective-permute-start(f32[32,8,128]{2,0,1:T(8,128)S(1)} %add.41), channel_id=1, source_target_pairs={{0,16},{16,0},{32,48},{48,32},{64,80},{80,64},{96,112},{112,96},{1... | collective-permute-start | bytes 393224 | tf_op jit(solution)/shard_map/ppermute | solution.py:270
